TPU v7x, 256 devices: a whole 4x4x8 slice. The times are simulated.
256 devices in a mesh: seq: 16 (over x, y_lo, core), emb: 16 (over y_hi, z).
Axes of the slice: x: 4, y: 4 (y_hi: 2, y_lo: 2; y = y_hi * 2 + y_lo), z: 8, core: 2. Of those that a mesh axis runs over, the one named last changes fastest.
Arguments:
- item_ids: int32 [131072], P('seq'), may hold values from 0 to 32767
- domains: int32 [131072], P(('seq', 'emb')), may hold values from 0 to 15, as said below
- live_counts: int32 [256], P(('seq', 'emb')), may hold values from 128 to 512, as said below
- table: bfloat16 [32768, 512], P(None, 'emb'), may hold values from -30 to 30
- norm_gains: float32 [3, 512], replicated, may hold values from 0.25 to 1.75
- proj_in: bfloat16 [512, 2048], replicated, may hold values from -0.25 to 0.25
- proj_out: bfloat16 [512, 512], replicated, may hold values from -0.25 to 0.25
- expert_in: bfloat16 [16, 512, 4096], P('emb'), may hold values from -0.25 to 0.25
- expert_out: bfloat16 [16, 2048, 512], P('emb'), may hold values from -0.125 to 0.125
Outputs:
- mixed: bfloat16 [131072, 512], P(('seq', 'emb'))
Inputs may be any that keep to these rules, and one draw needn't show every extreme that they name: `domains`: in the 512 events of one block no domain appears more than 64 times; in every group of 16 consecutive blocks some domain appears exactly 64 times in each block. `live_counts`: some block has all 512 events live.
All inputs are finite; a program needn't handle non-finite values.
Results may differ from a plain program's by a relative error of at most 0.006.
Values may be sent and summed in bfloat16 or wider, within the bound.
A program may use at most 128 MiB of HBM per device.

v0:
```python
import math

import jax
import jax.numpy as jnp
from jax import lax
from jax.sharding import PartitionSpec as P

HEADS = 8
HEAD_DIM = 64
SPAN = 4


norm_eps = 1e-06


def shifted(value, axis, steps):
    count = lax.axis_size(axis)
    first, last = (max(0, -steps), min(count, count - steps))
    return lax.ppermute(value, axis, [(source, source + steps) for source in range(first, last)])


def rms_norm(values, gain):
    return values * lax.rsqrt(jnp.mean(values * values, axis=-1, keepdims=True) + norm_eps) * gain


def body(
    item_ids, domains, live_counts, table, norm_gains, proj_in, proj_out, expert_in, expert_out
):
    rows_dev = domains.shape[0]
    model_width = proj_out.shape[0]
    hidden_units = expert_out.shape[1]
    group_size = lax.axis_size("emb")
    capacity = 2 * rows_dev // group_size
    columns = table[item_ids]
    embedded = lax.all_to_all(columns, "emb", split_axis=0, concat_axis=1, tiled=True).astype(
        jnp.float32
    )
    positions = jnp.arange(rows_dev, dtype=jnp.int32)
    live_mask = (positions < live_counts[0]).astype(jnp.float32)
    normed = (rms_norm(embedded, norm_gains[0]) * live_mask[:, None]).astype(jnp.bfloat16)
    projected = jnp.dot(normed, proj_in, preferred_element_type=jnp.float32)
    gating = jax.nn.silu(projected[:, :model_width])
    queries = (
        projected[:, model_width : 2 * model_width]
        .astype(jnp.bfloat16)
        .reshape(rows_dev, HEADS, HEAD_DIM)
    )
    own_pair = jnp.stack(
        (
            projected[:, 2 * model_width : 3 * model_width].astype(jnp.bfloat16),
            projected[:, 3 * model_width :].astype(jnp.bfloat16),
        )
    )
    key_weights = proj_in[:, 2 * model_width :]
    upper_band = positions[None, :] >= positions[:, None]
    lower_band = positions[None, :] <= positions[:, None]
    score_scale = 1.0 / math.sqrt(HEAD_DIM)

    def unpack(piece):
        rebuilt = jnp.dot(piece[0], key_weights, preferred_element_type=jnp.float32)
        return jnp.stack(
            (
                rebuilt[:, :model_width].astype(jnp.bfloat16),
                rebuilt[:, model_width:].astype(jnp.bfloat16),
            )
        )

    def attend(pair, band_mask):
        key_heads = pair[0].reshape(rows_dev, HEADS, HEAD_DIM)
        value_heads = pair[1].reshape(rows_dev, HEADS, HEAD_DIM)
        scores = (
            jnp.einsum("qhd,khd->hqk", queries, key_heads, preferred_element_type=jnp.float32)
            * score_scale
        )
        weights = jax.nn.silu(scores)
        if band_mask is not None:
            weights = jnp.where(band_mask[None], weights, 0.0)
        weights = weights.astype(jnp.bfloat16)
        return jnp.einsum(
            "hqk,khd->qhd", weights, value_heads, preferred_element_type=jnp.float32
        ).reshape(rows_dev, model_width)

    outgoing = normed[None]
    attended = attend(own_pair, None)
    earlier = outgoing
    following = outgoing
    for distance in range(1, SPAN + 1):
        band_before = upper_band if distance == SPAN else None
        band_after = lower_band if distance == SPAN else None
        earlier = shifted(earlier, ("seq", "emb"), 1)
        following = shifted(following, ("seq", "emb"), -1)
        attended = (
            attended + attend(unpack(earlier), band_before) + attend(unpack(following), band_after)
        )
    gated = (rms_norm(attended, norm_gains[1]) * gating).astype(jnp.bfloat16)
    hidden = embedded + jnp.dot(gated, proj_out, preferred_element_type=jnp.float32)
    routed = rms_norm(hidden, norm_gains[2]).astype(jnp.bfloat16)
    onehot_domain = (domains[:, None] == jnp.arange(group_size, dtype=jnp.int32)[None, :]).astype(
        jnp.int32
    )
    slot_rank = jnp.sum((jnp.cumsum(onehot_domain, axis=0) - onehot_domain) * onehot_domain, axis=1)
    slot_index = domains * capacity + slot_rank
    outgoing_rows = (
        jnp.zeros((group_size * capacity, model_width), jnp.bfloat16).at[slot_index].set(routed)
    )
    outgoing_rows = outgoing_rows.reshape(group_size, capacity, model_width)
    inbox = lax.all_to_all(outgoing_rows, "emb", split_axis=0, concat_axis=0, tiled=True)
    sources, slot_count, _ = inbox.shape
    flattened = inbox.reshape(sources * slot_count, model_width)
    gate_up = jnp.dot(flattened, expert_in[0], preferred_element_type=jnp.float32)
    activated = (jax.nn.silu(gate_up[:, :hidden_units]) * gate_up[:, hidden_units:]).astype(
        jnp.bfloat16
    )
    produced = jnp.dot(activated, expert_out[0], preferred_element_type=jnp.float32).astype(
        jnp.bfloat16
    )
    finished = produced.reshape(sources, slot_count, model_width)
    returned = lax.all_to_all(finished, "emb", split_axis=0, concat_axis=0, tiled=True).reshape(
        group_size * capacity, model_width
    )
    expert_rows = returned[slot_index].astype(jnp.float32)
    return (live_mask[:, None] * (hidden + expert_rows)).astype(jnp.bfloat16)


def solution(mesh):
    in_specs = (
        P("seq"),
        P(("seq", "emb")),
        P(("seq", "emb")),
        P(None, "emb"),
        P(),
        P(),
        P(),
        P("emb", None, None),
        P("emb", None, None),
    )
    out_specs = P(("seq", "emb"), None)
    return jax.shard_map(body, mesh=mesh, in_specs=in_specs, out_specs=out_specs, check_vma=False)
```

profile of v0, /device:TPU:12, one launch (start us, length us, event | category | flops | bytes accessed | tf_op | source)
XLA Modules:
  0.0 324.2 jit_solution(3991684145533057228)
XLA Ops:
  0.0 7.6 %copy.42 = bf16[32768,32]{1,0:T(8,128)(2,1)} copy(bf16[32768,32]{0,1:T(8,128)(2,1)} %param.12) | data formatting | bytes 4194304 | tf_op args[3]
  7.6 32.4 %gather_fusion = bf16[8192,32]{1,0:T(8,128)(2,1)} fusion(bf16[32768,32]{1,0:T(8,128)(2,1)} %copy.42, s32[8192]{0:T(1024)S(1)} %fusion.74), kind=kCustom, calls=%fused_computation | custom fusion | bytes 1081344 | tf_op jit(solution)/shard_map/gather | solution.py:34
  40.0 2.6 copy.43
  42.6 10.3 %all-to-all-start = ((bf16[16,512,32]{1,2,0:T(8,128)(2,1)}), bf16[16,512,32]{1,2,0:T(8,128)(2,1)S(1)}, u32[]{:S(2)}, u32[]{:S(2)}) async-start(bf16[16,512,32]{1,2,0:T(8,128)(2,1)} %copy.43), calls=%async_computation | async-start | bytes 1048576 | tf_op jit(solution)/shard_map/all_to_all | solution.py:35
  53.6 1.2 reduce-window.6
  56.0 14.1 %all-to-all-done = bf16[16,512,32]{1,2,0:T(8,128)(2,1)S(1)} async-done(((bf16[16,512,32]{1,2,0:T(8,128)(2,1)}), bf16[16,512,32]{1,2,0:T(8,128)(2,1)S(1)}, u32[]{:S(2)}, u32[]{:S(2)}) %all-to-all-start) | async-done | bytes 524320 | tf_op jit(solution)/shard_map/all_to_all | solution.py:35
  70.4 1.1 fusion.48
  71.5 3.0 collective-permute-start
  74.5 5.0 %collective-permute-start.1 = (bf16[1,512,512]{1,2,0:T(8,128)(2,1)}, bf16[1,512,512]{1,2,0:T(8,128)(2,1)}, u32[]{:S(2)}, u32[]{:S(2)}) collective-permute-start(bf16[1,512,512]{1,2,0:T(8,128)(2,1)} %fusion.48), channel_id=1, source_target_pairs={{1,0},{2,1},{3,2},{4,3},{5,4},{6,5},{7,6},{8,7},{9,8},{10,9},{11,1... | collective-permute-start | bytes 1572872 | tf_op jit(solution)/shard_map/ppermute | solution.py:19
  79.7 4.8 %fusion.112 = (bf16[512,2048]{1,0:T(8,128)(2,1)S(1)}, f32[512,2048]{1,0:T(8,128)}) fusion(bf16[512,512]{0,1:T(8,128)(2,1)S(1)} %fusion.52, bf16[512,2048]{1,0:T(8,128)(2,1)} %param.14), kind=kOutput, calls=%fused_computation.142 | convolution fusion | flops 1074790400 | bytes 8912896 | tf_op jit(solution)/shard_map/dot_general | solution.py:41
  85.4 2.1 copy.45
  88.7 5.9 %fusion.3 = f32[8,64,512]{2,1,0:T(8,128)} fusion(bf16[512,8,64]{0,2,1:T(8,128)(2,1)} %bitcast.170, bf16[512,8,64]{0,2,1:T(8,128)(2,1)} %bitcast.146, bf16[512,8,64]{0,2,1:T(8,128)(2,1)S(1)} %bitcast.172), kind=kOutput, calls=%fused_computation.16 | convolution fusion | flops 549453824 | bytes 2621440 | tf_op jit(solution)/shard_map/hqk,khd->qhd/dot_general | solution.py:79
  94.6 2.1 convolution_convert_fusion.7
  96.8 1.1 copy.47
  97.9 1.0 copy.48
  98.9 2.1 convolution_convert_fusion.6
  101.1 1.0 copy.49
  103.1 6.5 %fusion.43 = f32[8,64,512]{2,1,0:T(8,128)} fusion(f32[8,64,512]{2,1,0:T(8,128)} %fusion.3, bf16[512,8,64]{0,2,1:T(8,128)(2,1)} %bitcast.158, bf16[512,8,64]{0,2,1:T(8,128)(2,1)} %bitcast.147, bf16[512,8,64]{0,2,1:T(8,128)(2,1)} %bitcast.161), kind=kOutput, calls=%fused_computation.51 | convolution fusion | flops 549715968 | bytes 3670016 | tf_op jit(solution)/shard_map/hqk,khd->qhd/dot_general | solution.py:79
  109.6 2.4 collective-permute-start.2
  112.1 6.1 %fusion.42 = f32[8,64,512]{2,1,0:T(8,128)} fusion(f32[8,64,512]{2,1,0:T(8,128)} %fusion.43, bf16[512,8,64]{0,2,1:T(8,128)(2,1)S(1)} %bitcast.163, bf16[512,8,64]{0,2,1:T(8,128)(2,1)S(1)} %bitcast.152, bf16[512,8,64]{0,2,1:T(8,128)(2,1)} %bitcast.165), kind=kOutput, calls=%fused_computation.50 | convolution fusion | flops 549715968 | bytes 3670016 | tf_op jit(solution)/shard_map/hqk,khd->qhd/dot_general | solution.py:79
  118.2 5.7 %collective-permute-start.3 = (bf16[1,512,512]{1,2,0:T(8,128)(2,1)}, bf16[1,512,512]{1,2,0:T(8,128)(2,1)}, u32[]{:S(2)}, u32[]{:S(2)}) collective-permute-start(bf16[1,512,512]{1,2,0:T(8,128)(2,1)} %collective-permute-done.1), channel_id=1, source_target_pairs={{1,0},{2,1},{3,2},{4,3},{5,4},{6,5},{7,6},{8,7},{9,8},{10,9},{11,1... | collective-permute-start | bytes 1572872 | tf_op jit(solution)/shard_map/ppermute | solution.py:19
  123.9 4.6 %collective-permute-done.2 = bf16[1,512,512]{1,2,0:T(8,128)(2,1)} collective-permute-done((bf16[1,512,512]{1,2,0:T(8,128)(2,1)}, bf16[1,512,512]{1,2,0:T(8,128)(2,1)}, u32[]{:S(2)}, u32[]{:S(2)}) %collective-permute-start.2) | collective-permute-done | bytes 524320 | tf_op jit(solution)/shard_map/ppermute | solution.py:19
  128.5 2.1 convolution_convert_fusion.5
  130.7 1.0 copy.51
  131.7 1.0 copy.52
  132.8 3.7 %collective-permute-done.3 = bf16[1,512,512]{1,2,0:T(8,128)(2,1)} collective-permute-done((bf16[1,512,512]{1,2,0:T(8,128)(2,1)}, bf16[1,512,512]{1,2,0:T(8,128)(2,1)}, u32[]{:S(2)}, u32[]{:S(2)}) %collective-permute-start.3) | collective-permute-done | bytes 524320 | tf_op jit(solution)/shard_map/ppermute | solution.py:19
  136.5 2.1 convolution_convert_fusion.4
  138.7 1.0 copy.53
  139.7 1.0 copy.54
  140.7 6.5 %fusion.41 = f32[8,64,512]{2,1,0:T(8,128)} fusion(f32[8,64,512]{2,1,0:T(8,128)} %fusion.42, bf16[512,8,64]{0,2,1:T(8,128)(2,1)} %bitcast.159, bf16[512,8,64]{0,2,1:T(8,128)(2,1)} %bitcast.148, bf16[512,8,64]{0,2,1:T(8,128)(2,1)} %bitcast.162), kind=kOutput, calls=%fused_computation.49 | convolution fusion | flops 549715968 | bytes 3670016 | tf_op jit(solution)/shard_map/hqk,khd->qhd/dot_general | solution.py:79
  147.2 2.1 collective-permute-start.4
  149.3 6.1 %fusion.40 = f32[8,64,512]{2,1,0:T(8,128)} fusion(f32[8,64,512]{2,1,0:T(8,128)} %fusion.41, bf16[512,8,64]{0,2,1:T(8,128)(2,1)S(1)} %bitcast.164, bf16[512,8,64]{0,2,1:T(8,128)(2,1)S(1)} %bitcast.153, bf16[512,8,64]{0,2,1:T(8,128)(2,1)} %bitcast.166), kind=kOutput, calls=%fused_computation.48 | convolution fusion | flops 549715968 | bytes 3670016 | tf_op jit(solution)/shard_map/hqk,khd->qhd/dot_general | solution.py:79
  155.4 6.3 %collective-permute-start.5 = (bf16[1,512,512]{1,2,0:T(8,128)(2,1)}, bf16[1,512,512]{1,2,0:T(8,128)(2,1)}, u32[]{:S(2)}, u32[]{:S(2)}) collective-permute-start(bf16[1,512,512]{1,2,0:T(8,128)(2,1)} %collective-permute-done.3), channel_id=1, source_target_pairs={{1,0},{2,1},{3,2},{4,3},{5,4},{6,5},{7,6},{8,7},{9,8},{10,9},{11,1... | collective-permute-start | bytes 1572872 | tf_op jit(solution)/shard_map/ppermute | solution.py:19
  161.8 4.6 %collective-permute-done.4 = bf16[1,512,512]{1,2,0:T(8,128)(2,1)} collective-permute-done((bf16[1,512,512]{1,2,0:T(8,128)(2,1)}, bf16[1,512,512]{1,2,0:T(8,128)(2,1)}, u32[]{:S(2)}, u32[]{:S(2)}) %collective-permute-start.4) | collective-permute-done | bytes 524320 | tf_op jit(solution)/shard_map/ppermute | solution.py:19
  166.4 2.1 convolution_convert_fusion.3
  168.6 1.0 copy.55
  169.8 6.2 %fusion.39 = f32[8,64,512]{2,1,0:T(8,128)} fusion(f32[8,64,512]{2,1,0:T(8,128)} %fusion.40, bf16[512,8,64]{0,2,1:T(8,128)(2,1)} %bitcast.169, bf16[512,8,64]{0,2,1:T(8,128)(2,1)} %bitcast.149, bf16[512,8,64]{0,2,1:T(8,128)(2,1)S(1)} %bitcast.171), kind=kOutput, calls=%fused_computation.47 | convolution fusion | flops 549715968 | bytes 3670016 | tf_op jit(solution)/shard_map/hqk,khd->qhd/dot_general | solution.py:79
  176.1 1.9 collective-permute-start.6
  178.0 2.1 convolution_convert_fusion.2
  180.2 1.0 copy.57
  181.2 1.0 copy.58
  182.2 6.0 %collective-permute-start.7 = (bf16[1,512,512]{1,2,0:T(8,128)(2,1)}, bf16[1,512,512]{1,2,0:T(8,128)(2,1)}, u32[]{:S(2)}, u32[]{:S(2)}) collective-permute-start(bf16[1,512,512]{1,2,0:T(8,128)(2,1)} %collective-permute-done.5), channel_id=1, source_target_pairs={{1,0},{2,1},{3,2},{4,3},{5,4},{6,5},{7,6},{8,7},{9,8},{10,9},{11,1... | collective-permute-start | bytes 1572872 | tf_op jit(solution)/shard_map/ppermute | solution.py:19
  188.2 5.7 %collective-permute-done.6 = bf16[1,512,512]{1,2,0:T(8,128)(2,1)} collective-permute-done((bf16[1,512,512]{1,2,0:T(8,128)(2,1)}, bf16[1,512,512]{1,2,0:T(8,128)(2,1)}, u32[]{:S(2)}, u32[]{:S(2)}) %collective-permute-start.6) | collective-permute-done | bytes 524320 | tf_op jit(solution)/shard_map/ppermute | solution.py:19
  193.9 2.1 convolution_convert_fusion.1
  197.1 1.1 copy.60
  198.1 2.1 convolution_convert_fusion
  200.3 1.0 copy.61
  201.4 1.0 copy.62
  202.4 6.1 %fusion.10 = f32[8,64,512]{2,1,0:T(8,128)} fusion(bf16[512,8,64]{0,2,1:T(8,128)(2,1)} %bitcast.157, pred[512,512]{1,0:T(8,128)(4,1)} %iota_compare_fusion.1, bf16[512,8,64]{0,2,1:T(8,128)(2,1)} %bitcast.150, bf16[512,8,64]{0,2,1:T(8,128)(2,1)} %bitcast.160), kind=kOutput, calls=%fused_computation.23 | convolution fusion | flops 551550976 | bytes 2883584 | tf_op jit(solution)/shard_map/hqk,khd->qhd/dot_general | solution.py:79
  208.5 5.7 %fusion.11 = f32[8,64,512]{2,1,0:T(8,128)} fusion(bf16[512,8,64]{0,2,1:T(8,128)(2,1)S(1)} %bitcast.167, pred[512,512]{1,0:T(8,128)(4,1)S(1)} %iota_compare_fusion, bf16[512,8,64]{0,2,1:T(8,128)(2,1)S(1)} %bitcast.154, bf16[512,8,64]{0,2,1:T(8,128)(2,1)} %bitcast.168), kind=kOutput, calls=%fused_computation.24 | convolution fusion | flops 551550976 | bytes 2883584 | tf_op jit(solution)/shard_map/hqk,khd->qhd/dot_general | solution.py:79
  214.2 7.4 %fusion.49 = (f32[512]{0:T(512)S(1)}, f32[8,64,512]{2,1,0:T(8,128)}) fusion(f32[8,64,512]{2,1,0:T(8,128)} %fusion.11, f32[8,64,512]{2,1,0:T(8,128)} %fusion.10, f32[8,64,512]{2,1,0:T(8,128)} %fusion.39, bf16[512,8,64]{0,2,1:T(8,128)(2,1)} %bitcast.155, bf16[512,8,64]{0,2,1:T(8,128)(2,1)} %bitcast.151, bf16[512,8,64]{0,2,1:T(8,128)(2,1)} %bitcast.156), kind=kOutput, calls=%fused_computation.59 | convolution fusion | flops 550764032 | bytes 5769216 | tf_op jit(solution)/shard_map/hqk,khd->qhd/dot_general | solution.py:79
  221.7 2.6 copy.63
  224.3 2.4 multiply_reduce_fusion
  227.8 1.0 copy.65
  228.8 3.2 scatter_custom_fusion
  232.0 41.5 %all_to_all.23 = bf16[16,64,512]{2,1,0:T(8,128)(2,1)S(1)} all-to-all(bf16[16,64,512]{2,1,0:T(8,128)(2,1)S(1)} %bitcast.142), channel_id=1, replica_groups=mesh['seq'=16,'emb'=16] {'emb'}, dimensions={0} | all-to-all | bytes 2097152 | tf_op jit(solution)/shard_map/all_to_all | solution.py:107
  273.6 6.3 %fusion.1 = f32[1024,4096]{1,0:T(8,128)S(1)} fusion(bf16[1024,512]{1,0:T(8,128)(2,1)S(1)} %bitcast.145, bf16[1,512,4096]{2,1,0:T(8,128)(2,1)} %param.16), kind=kOutput, calls=%fused_computation.14 | convolution fusion | flops 4294967296 | bytes 22020096 | tf_op jit(solution)/shard_map/dot_general | solution.py:110
  279.9 3.5 %fusion.33 = bf16[1024,512]{1,0:T(8,128)(2,1)} fusion(bf16[1,2048,512]{2,1,0:T(8,128)(2,1)S(1)} %copy-done, f32[1024,4096]{1,0:T(8,128)S(1)} %fusion.1), kind=kOutput, calls=%fused_computation.36 | convolution fusion | flops 2160590848 | bytes 19922944 | tf_op jit(solution)/shard_map/dot_general | solution.py:114
  283.4 5.3 %all-to-all-start.2 = ((bf16[16,64,512]{2,1,0:T(8,128)(2,1)}), bf16[16,64,512]{2,1,0:T(8,128)(2,1)S(1)}, u32[]{:S(2)}, u32[]{:S(2)}) async-start(bf16[16,64,512]{2,1,0:T(8,128)(2,1)} %bitcast.144), calls=%async_computation.2 | async-start | bytes 2097152 | tf_op jit(solution)/shard_map/all_to_all | solution.py:118
  288.8 28.9 %all-to-all-done.2 = bf16[16,64,512]{2,1,0:T(8,128)(2,1)S(1)} async-done(((bf16[16,64,512]{2,1,0:T(8,128)(2,1)}), bf16[16,64,512]{2,1,0:T(8,128)(2,1)S(1)}, u32[]{:S(2)}, u32[]{:S(2)}) %all-to-all-start.2) | async-done | bytes 1048608 | tf_op jit(solution)/shard_map/all_to_all | solution.py:118
  317.7 2.6 gather_fusion.1
  320.3 1.3 copy.66
  321.5 1.4 multiply_convert_fusion.30
  322.9 1.0 copy.67
  (67 shorter events, 7.9 us)
Async XLA Ops:
  0.0 279.9 %copy-start = (bf16[1,2048,512]{2,1,0:T(8,128)(2,1)S(1)}, bf16[1,2048,512]{2,1,0:T(8,128)(2,1)}, u32[]{:S(2)}) copy-start(bf16[1,2048,512]{2,1,0:T(8,128)(2,1)} %param.17) | copy-start | bytes 6291460
  0.0 7.6 %copy-start.12 = (s32[8192]{0:T(1024)S(1)}, s32[8192]{0:T(1024)}, u32[]{:S(2)}) copy-start(s32[8192]{0:T(1024)} %param.9) | copy-start | bytes 98308
  7.6 46.0 %copy-start.13 = (s32[512]{0:T(512)S(1)}, s32[512]{0:T(512)}, u32[]{:S(2)}) copy-start(s32[512]{0:T(512)} %param.10) | copy-start | bytes 6148
  7.6 48.4 %copy-start.14 = (f32[3,512]{1,0:T(4,128)S(1)}, f32[3,512]{1,0:T(4,128)}, u32[]{:S(2)}) copy-start(f32[3,512]{1,0:T(4,128)} %param.13) | copy-start | bytes 18436
  42.6 27.5 %all-to-all-start = ((bf16[16,512,32]{1,2,0:T(8,128)(2,1)}), bf16[16,512,32]{1,2,0:T(8,128)(2,1)S(1)}, u32[]{:S(2)}, u32[]{:S(2)}) async-start(bf16[16,512,32]{1,2,0:T(8,128)(2,1)} %copy.43), calls=%async_computation | async-start | bytes 1048576 | tf_op jit(solution)/shard_map/all_to_all | solution.py:35
  55.0 29.5 %copy-start.10 = (f32[512]{0:T(512)}, f32[512]{0:T(512)S(1)}, u32[]{:S(2)}) copy-start(f32[512]{0:T(512)S(1)} %fusion.79) | copy-start | bytes 6148
  70.4 9.1 %copy-start.2 = (f32[16,512,32]{1,2,0:T(8,128)}, f32[16,512,32]{1,2,0:T(8,128)S(1)}, u32[]{:S(2)}) copy-start(f32[16,512,32]{1,2,0:T(8,128)S(1)} %convert_element_type.144) | copy-start | bytes 3145732
  71.5 23.1 %collective-permute-start = (bf16[1,512,512]{1,2,0:T(8,128)(2,1)}, bf16[1,512,512]{1,2,0:T(8,128)(2,1)}, u32[]{:S(2)}, u32[]{:S(2)}) collective-permute-start(bf16[1,512,512]{1,2,0:T(8,128)(2,1)} %fusion.48), channel_id=1, source_target_pairs={{0,1},{1,2},{2,3},{3,4},{4,5},{5,6},{6,7},{7,8},{8,9},{9,10},{10,1... | collective-permute-start | bytes 1572872 | tf_op jit(solution)/shard_map/ppermute | solution.py:19
  74.5 24.5 %collective-permute-start.1 = (bf16[1,512,512]{1,2,0:T(8,128)(2,1)}, bf16[1,512,512]{1,2,0:T(8,128)(2,1)}, u32[]{:S(2)}, u32[]{:S(2)}) collective-permute-start(bf16[1,512,512]{1,2,0:T(8,128)(2,1)} %fusion.48), channel_id=1, source_target_pairs={{1,0},{2,1},{3,2},{4,3},{5,4},{6,5},{7,6},{8,7},{9,8},{10,9},{11,1... | collective-permute-start | bytes 1572872 | tf_op jit(solution)/shard_map/ppermute | solution.py:19
  103.1 8.9 %copy-start.4 = (bf16[512,512]{0,1:T(8,128)(2,1)S(1)}, bf16[512,512]{0,1:T(8,128)(2,1)}, u32[]{:S(2)}) copy-start(bf16[512,512]{0,1:T(8,128)(2,1)} %copy.45) | copy-start | bytes 1572868
  103.1 8.9 %copy-start.7 = (bf16[512,512]{0,1:T(8,128)(2,1)S(1)}, bf16[512,512]{0,1:T(8,128)(2,1)}, u32[]{:S(2)}) copy-start(bf16[512,512]{0,1:T(8,128)(2,1)} %copy.49) | copy-start | bytes 1572868
  109.6 18.9 %collective-permute-start.2 = (bf16[1,512,512]{1,2,0:T(8,128)(2,1)}, bf16[1,512,512]{1,2,0:T(8,128)(2,1)}, u32[]{:S(2)}, u32[]{:S(2)}) collective-permute-start(bf16[1,512,512]{1,2,0:T(8,128)(2,1)} %collective-permute-done), channel_id=1, source_target_pairs={{0,1},{1,2},{2,3},{3,4},{4,5},{5,6},{6,7},{7,8},{8,9},{9,10},{10,1... | collective-permute-start | bytes 1572872 | tf_op jit(solution)/shard_map/ppermute | solution.py:19
  118.2 18.3 %collective-permute-start.3 = (bf16[1,512,512]{1,2,0:T(8,128)(2,1)}, bf16[1,512,512]{1,2,0:T(8,128)(2,1)}, u32[]{:S(2)}, u32[]{:S(2)}) collective-permute-start(bf16[1,512,512]{1,2,0:T(8,128)(2,1)} %collective-permute-done.1), channel_id=1, source_target_pairs={{1,0},{2,1},{3,2},{4,3},{5,4},{6,5},{7,6},{8,7},{9,8},{10,9},{11,1... | collective-permute-start | bytes 1572872 | tf_op jit(solution)/shard_map/ppermute | solution.py:19
  140.7 8.6 %copy-start.5 = (bf16[512,512]{0,1:T(8,128)(2,1)S(1)}, bf16[512,512]{0,1:T(8,128)(2,1)}, u32[]{:S(2)}) copy-start(bf16[512,512]{0,1:T(8,128)(2,1)} %copy.45) | copy-start | bytes 1572868
  140.7 8.6 %copy-start.8 = (bf16[512,512]{0,1:T(8,128)(2,1)S(1)}, bf16[512,512]{0,1:T(8,128)(2,1)}, u32[]{:S(2)}) copy-start(bf16[512,512]{0,1:T(8,128)(2,1)} %copy.53) | copy-start | bytes 1572868
  147.2 19.2 %collective-permute-start.4 = (bf16[1,512,512]{1,2,0:T(8,128)(2,1)}, bf16[1,512,512]{1,2,0:T(8,128)(2,1)}, u32[]{:S(2)}, u32[]{:S(2)}) collective-permute-start(bf16[1,512,512]{1,2,0:T(8,128)(2,1)} %collective-permute-done.2), channel_id=1, source_target_pairs={{0,1},{1,2},{2,3},{3,4},{4,5},{5,6},{6,7},{7,8},{8,9},{9,10},{10,1... | collective-permute-start | bytes 1572872 | tf_op jit(solution)/shard_map/ppermute | solution.py:19
  155.4 22.5 %collective-permute-start.5 = (bf16[1,512,512]{1,2,0:T(8,128)(2,1)}, bf16[1,512,512]{1,2,0:T(8,128)(2,1)}, u32[]{:S(2)}, u32[]{:S(2)}) collective-permute-start(bf16[1,512,512]{1,2,0:T(8,128)(2,1)} %collective-permute-done.3), channel_id=1, source_target_pairs={{1,0},{2,1},{3,2},{4,3},{5,4},{6,5},{7,6},{8,7},{9,8},{10,9},{11,1... | collective-permute-start | bytes 1572872 | tf_op jit(solution)/shard_map/ppermute | solution.py:19
  176.1 17.8 %collective-permute-start.6 = (bf16[1,512,512]{1,2,0:T(8,128)(2,1)}, bf16[1,512,512]{1,2,0:T(8,128)(2,1)}, u32[]{:S(2)}, u32[]{:S(2)}) collective-permute-start(bf16[1,512,512]{1,2,0:T(8,128)(2,1)} %collective-permute-done.4), channel_id=1, source_target_pairs={{0,1},{1,2},{2,3},{3,4},{4,5},{5,6},{6,7},{7,8},{8,9},{9,10},{10,1... | collective-permute-start | bytes 1572872 | tf_op jit(solution)/shard_map/ppermute | solution.py:19
  182.2 15.9 %collective-permute-start.7 = (bf16[1,512,512]{1,2,0:T(8,128)(2,1)}, bf16[1,512,512]{1,2,0:T(8,128)(2,1)}, u32[]{:S(2)}, u32[]{:S(2)}) collective-permute-start(bf16[1,512,512]{1,2,0:T(8,128)(2,1)} %collective-permute-done.5), channel_id=1, source_target_pairs={{1,0},{2,1},{3,2},{4,3},{5,4},{6,5},{7,6},{8,7},{9,8},{10,9},{11,1... | collective-permute-start | bytes 1572872 | tf_op jit(solution)/shard_map/ppermute | solution.py:19
  202.4 6.1 %copy-start.6 = (bf16[512,512]{0,1:T(8,128)(2,1)S(1)}, bf16[512,512]{0,1:T(8,128)(2,1)}, u32[]{:S(2)}) copy-start(bf16[512,512]{0,1:T(8,128)(2,1)} %copy.45) | copy-start | bytes 1572868
  202.4 6.1 %copy-start.9 = (bf16[512,512]{0,1:T(8,128)(2,1)S(1)}, bf16[512,512]{0,1:T(8,128)(2,1)}, u32[]{:S(2)}) copy-start(bf16[512,512]{0,1:T(8,128)(2,1)} %copy.61) | copy-start | bytes 1572868
  214.2 10.0 %copy-start.3 = (f32[16,512,32]{1,2,0:T(8,128)S(1)}, f32[16,512,32]{1,2,0:T(8,128)}, u32[]{:S(2)}) copy-start(f32[16,512,32]{1,2,0:T(8,128)} %copy-done.2) | copy-start | bytes 3145732
  226.7 1.0 copy-start.1
  279.9 41.6 %copy-start.11 = (f32[512]{0:T(512)S(1)}, f32[512]{0:T(512)}, u32[]{:S(2)}) copy-start(f32[512]{0:T(512)} %copy-done.10) | copy-start | bytes 6148
  283.4 34.2 %all-to-all-start.2 = ((bf16[16,64,512]{2,1,0:T(8,128)(2,1)}), bf16[16,64,512]{2,1,0:T(8,128)(2,1)S(1)}, u32[]{:S(2)}, u32[]{:S(2)}) async-start(bf16[16,64,512]{2,1,0:T(8,128)(2,1)} %bitcast.144), calls=%async_computation.2 | async-start | bytes 2097152 | tf_op jit(solution)/shard_map/all_to_all | solution.py:118
where the time goes:
time: 328 us; the launch traced here: 324 us
  matrix products  90.5 us (28%)
  local copies, waits for them, and re-layouts  75.9 us (23%)
  waiting for transfers between devices  61.7 us (19%)
  starting transfers between devices  48 us (15%)
  blocking collectives  41.5 us (13%)
  other arithmetic  5.29 us (2%)
    dot_general x9, matrix products, attend(): jnp.einsum('hqk,khd->qhd', weights, value_heads, preferred_element_type=j...  56.5 us
    all_to_all x1, blocking collectives, body(): lax.all_to_all(outgoing_rows, 'emb', split_axis=0, concat_axis=0, tiled=T...  41.5 us
    gather x1, local copies, waits for them, and re-layouts, body(): columns = table[item_ids]  32.4 us
    ppermute x8, starting transfers between devices, shifted(): lax.ppermute(value, axis, [(source, source + steps) for source in range(f...  32.4 us
    all_to_all x1, waiting for transfers between devices, body(): lax.all_to_all(finished, 'emb', split_axis=0, concat_axis=0, tiled=True)  28.9 us
    ppermute x8, waiting for transfers between devices, shifted(): lax.ppermute(value, axis, [(source, source + steps) for source in range(f...  18.7 us
    dot_general x8, matrix products, unpack(): rebuilt = jnp.dot(piece[0], key_weights, preferred_element_type=jnp.float32)  16.9 us
    all_to_all x1, waiting for transfers between devices, body(): lax.all_to_all(columns, 'emb', split_axis=0, concat_axis=1, tiled=True)  14.1 us
  transfers between devices with their start and end apart: 10, of which 6 were waited for; matrix products, arithmetic and copies ran while one was open for 17% of the time, Pallas kernels for 0%

commit v1 on v0

v1 whole, which is shorter than its diff:
```python
import math

import jax
import jax.numpy as jnp
from jax import lax
from jax.experimental import pallas as pl
from jax.experimental.pallas import tpu as pltpu
from jax.sharding import PartitionSpec as P

HEADS = 8
HEAD_DIM = 64
SPAN = 4
MESH = pl.DeviceIdType.MESH

norm_eps = 1e-06

ORDER = (4, 12, 3, 13, 5, 11, 2, 14, 6, 10, 1, 15, 7, 9, 8, 0)


def rms_norm(values, gain):
    return values * lax.rsqrt(jnp.mean(values * values, axis=-1, keepdims=True) + norm_eps) * gain


def silu(values):
    return values * (0.5 * jnp.tanh(0.5 * values) + 0.5)


def attention_kernel(
    normed_ref, embedded_ref, gains_ref, proj_in_ref, proj_out_ref, slot_ref,
    hidden_ref, outgoing_ref,
    halo, queries, gating, keys, values, total, send_sem, recv_sem,
):
    rows, width = normed_ref.shape
    half = rows // 2
    pairs = width // 128
    groups, members = lax.axis_size("seq"), lax.axis_size("emb")
    count = groups * members
    me = lax.axis_index("seq") * members + lax.axis_index("emb")
    right = lax.rem(me + 1, count)
    left = lax.rem(me + count - 1, count)
    targets = [
        (lax.div(right, members), lax.rem(right, members)),
        (lax.div(left, members), lax.rem(left, members)),
    ]

    barrier = pltpu.get_barrier_semaphore()
    for target in targets:
        pl.semaphore_signal(barrier, inc=1, device_id=target, device_id_type=MESH)
    pl.semaphore_wait(barrier, 2)

    def transfer(way, distance, part, source):
        slot = (way, distance, part)
        return pltpu.make_async_remote_copy(
            src_ref=source,
            dst_ref=halo.at[slot],
            send_sem=send_sem.at[slot],
            recv_sem=recv_sem.at[slot],
            device_id=targets[way],
            device_id_type=MESH,
        )

    for part in range(2):
        for way in range(2):
            transfer(way, 0, part, normed_ref.at[pl.ds(part * half, half)]).start()

    normed = normed_ref[...]
    for pair in range(pairs):
        columns = pl.ds(pair * 128, 128)
        gate = jnp.dot(normed, proj_in_ref[:, columns], preferred_element_type=jnp.float32)
        gating[:, columns] = silu(gate)
        query = jnp.dot(
            normed, proj_in_ref[:, pl.ds(width + pair * 128, 128)], preferred_element_type=jnp.float32
        ).astype(jnp.bfloat16)
        queries[pair] = query * jnp.bfloat16(0.5 / math.sqrt(HEAD_DIM))
        total[pair] = jnp.zeros((rows, 128), jnp.float32)

    low_lanes = lax.broadcasted_iota(jnp.int32, (half, 128), 1) < HEAD_DIM

    def attend(block, tiles):
        def project(pair, carry):
            for base, held in ((2 * width, keys), (3 * width, values)):
                columns = pl.ds(pl.multiple_of(base + pair * 128, 128), 128)
                found = jnp.dot(block, proj_in_ref[:, columns], preferred_element_type=jnp.float32)
                held[pair, pl.ds(0, half), :] = jnp.where(low_lanes, found, 0.0).astype(jnp.bfloat16)
                held[pair, pl.ds(half, half), :] = jnp.where(low_lanes, 0.0, found).astype(jnp.bfloat16)
            return carry

        lax.fori_loop(0, pairs, project, 0)

        def weigh(pair, carry):
            for tile, band in tiles:
                span = pl.ds(tile * half, half)
                scores = lax.dot_general(
                    queries[pair, span, :], keys[pair], (((1,), (1,)), ((), ())),
                    preferred_element_type=jnp.float32,
                )
                weights = scores * jnp.tanh(scores) + scores
                if band is not None:
                    row = lax.broadcasted_iota(jnp.int32, scores.shape, 0)
                    column = lax.broadcasted_iota(jnp.int32, scores.shape, 1) & (half - 1)
                    weights = jnp.where(column >= row if band == 0 else column <= row, weights, 0.0)
                total[pair, span, :] += jnp.dot(
                    weights.astype(jnp.bfloat16), values[pair], preferred_element_type=jnp.float32
                )
            return carry

        lax.fori_loop(0, pairs, weigh, 0)

    everything = ((0, None), (1, None))

    def own(part, carry):
        attend(normed_ref[pl.ds(pl.multiple_of(part * half, half), half), :], everything)
        return carry

    lax.fori_loop(0, 2, own, 0)

    def in_range(way, distance):
        return me - distance > 0 if way == 0 else me + distance < count - 1

    def step(index, carry):
        distance, part = lax.div(index, 2), lax.rem(index, 2)
        for way in range(2):
            arrived = halo.at[way, distance, part]
            transfer(way, distance, part, arrived).wait_recv()
            transfer(way, distance + 1, part, arrived).start()

        def one(way, carry):
            inside = jnp.where(way == 0, me - distance > 0, me + distance < count - 1)

            @pl.when(inside)
            def _():
                attend(halo[way, distance, part], everything)

            return carry

        lax.fori_loop(0, 2, one, 0)
        return carry

    lax.fori_loop(0, 2 * (SPAN - 1), step, 0)

    last = SPAN - 1
    edge_tiles = (
        (((0, 0),), ((0, 1), (1, None))),
        (((0, None), (1, 0)), ((1, 1),)),
    )
    for part in range(2):
        for way in range(2):
            transfer(way, last, part, halo.at[way, last, part]).wait_recv()

            @pl.when(in_range(way, last))
            def _():
                attend(halo[way, last, part], edge_tiles[part][way])

    def settle(index, carry):
        distance, part = lax.div(index, 2), lax.rem(index, 2)
        for way in range(2):
            transfer(way, distance, part, halo.at[way, distance, part]).wait_send()
        return carry

    lax.fori_loop(0, 2 * SPAN, settle, 0)

    attended = jnp.concatenate([total[pair] for pair in range(pairs)], axis=1)
    gated = (rms_norm(attended, gains_ref[1:2, :]) * gating[...]).astype(jnp.bfloat16)
    hidden = embedded_ref[...].astype(jnp.float32) + jnp.dot(
        gated, proj_out_ref[...], preferred_element_type=jnp.float32
    )
    hidden_ref[...] = hidden
    routed = rms_norm(hidden, gains_ref[2:3, :]).astype(jnp.bfloat16)
    slots = outgoing_ref.shape[0]
    chunk = 256
    for first in range(0, slots, chunk):
        number = lax.broadcasted_iota(jnp.int32, (chunk, rows), 0) + first
        chosen = jnp.where(number == slot_ref[...], 1.0, 0.0).astype(jnp.bfloat16)
        outgoing_ref[pl.ds(first, chunk), :] = jnp.dot(
            chosen, routed, preferred_element_type=jnp.float32
        ).astype(jnp.bfloat16)


def expert_kernel(
    live_ref, outgoing_ref, slot_ref, hidden_ref, expert_in_ref, expert_out_ref,
    mixed_ref,
    up, down, inbox, finished, returned, load_sem, send_sem, recv_sem, back_send, back_recv,
):
    members, capacity, width = outgoing_ref.shape
    hidden_units = down.shape[0]
    rows = hidden_ref.shape[0]
    group = lax.axis_index("seq")
    me = lax.axis_index("emb")

    loads = [
        pltpu.make_async_copy(expert_in_ref.at[0], up, load_sem.at[0]),
        pltpu.make_async_copy(expert_out_ref.at[0], down, load_sem.at[1]),
    ]
    for load in loads:
        load.start()

    barrier = pltpu.get_barrier_semaphore()
    for offset in range(1, members):
        pl.semaphore_signal(
            barrier, inc=1, device_id=(group, lax.rem(me + offset, members)), device_id_type=MESH
        )
    pl.semaphore_wait(barrier, members - 1)

    def dispatch(place):
        target = lax.rem(me + ORDER[place], members)
        return pltpu.make_async_remote_copy(
            src_ref=outgoing_ref.at[target],
            dst_ref=inbox.at[place],
            send_sem=send_sem.at[place],
            recv_sem=recv_sem.at[place],
            device_id=(group, target),
            device_id_type=MESH,
        )

    def give_back(place):
        target = lax.rem(me + members - ORDER[place], members)
        return pltpu.make_async_remote_copy(
            src_ref=finished.at[place],
            dst_ref=returned.at[me],
            send_sem=back_send.at[place],
            recv_sem=back_recv.at[place],
            device_id=(group, target),
            device_id_type=MESH,
        )

    remote = [place for place in range(members) if ORDER[place] != 0]
    home = ORDER.index(0)
    for place in remote:
        dispatch(place).start()
    inbox[home] = outgoing_ref[me]

    batch = 4
    tile = 256
    for load in loads:
        load.wait()
    for first in range(0, members, batch):
        places = [place for place in range(first, first + batch) if place != home]
        for place in places:
            dispatch(place).wait_recv()
        taken = inbox[pl.ds(first, batch)].reshape(batch * capacity, width)

        def expert(index, result):
            start = pl.multiple_of(index * tile, tile)
            gate = jnp.dot(taken, up[:, pl.ds(start, tile)], preferred_element_type=jnp.float32)
            lift = jnp.dot(
                taken, up[:, pl.ds(pl.multiple_of(hidden_units + start, tile), tile)],
                preferred_element_type=jnp.float32,
            )
            activated = (silu(gate) * lift).astype(jnp.bfloat16)
            return result + jnp.dot(
                activated, down[pl.ds(start, tile), :], preferred_element_type=jnp.float32
            )

        produced = lax.fori_loop(
            0, hidden_units // tile, expert, jnp.zeros((batch * capacity, width), jnp.float32)
        ).astype(jnp.bfloat16)
        finished[pl.ds(first, batch)] = produced.reshape(batch, capacity, width)
        for place in places:
            give_back(place).start()

    returned[me] = finished[home]
    for place in remote:
        give_back(place).wait_recv()

    number = lax.broadcasted_iota(jnp.int32, (rows, members * capacity), 1)
    chosen = jnp.where(number == slot_ref[...], 1.0, 0.0).astype(jnp.bfloat16)
    expert_rows = jnp.dot(
        chosen, returned[...].reshape(members * capacity, width), preferred_element_type=jnp.float32
    )
    live = lax.broadcasted_iota(jnp.int32, (rows, width), 0) < live_ref[0]
    mixed_ref[...] = jnp.where(live, hidden_ref[...] + expert_rows, 0.0).astype(jnp.bfloat16)
    for place in remote:
        dispatch(place).wait_send()
        give_back(place).wait_send()


VMEM = pl.BlockSpec(memory_space=pltpu.VMEM)


def body(
    item_ids, domains, live_counts, table, norm_gains, proj_in, proj_out, expert_in, expert_out
):
    rows = domains.shape[0]
    width = proj_out.shape[0]
    hidden_units = expert_out.shape[1]
    members = lax.axis_size("emb")
    capacity = 2 * rows // members
    slots = members * capacity

    onehot_domain = (domains[:, None] == jnp.arange(members, dtype=jnp.int32)[None, :]).astype(jnp.int32)
    slot_rank = jnp.sum((jnp.cumsum(onehot_domain, axis=0) - onehot_domain) * onehot_domain, axis=1)
    slot_index = domains * capacity + slot_rank

    columns = table[item_ids]
    embedded = lax.all_to_all(columns, "emb", split_axis=0, concat_axis=1, tiled=True)
    positions = jnp.arange(rows, dtype=jnp.int32)
    live_mask = (positions < live_counts[0]).astype(jnp.float32)
    normed = (rms_norm(embedded.astype(jnp.float32), norm_gains[0]) * live_mask[:, None]).astype(jnp.bfloat16)

    half = rows // 2
    pairs = width // 128
    hidden, outgoing = pl.pallas_call(
        attention_kernel,
        out_shape=(
            jax.ShapeDtypeStruct((rows, width), jnp.float32),
            jax.ShapeDtypeStruct((slots, width), jnp.bfloat16),
        ),
        in_specs=[VMEM] * 6,
        out_specs=(VMEM, VMEM),
        scratch_shapes=[
            pltpu.VMEM((2, SPAN, 2, half, width), jnp.bfloat16),
            pltpu.VMEM((pairs, rows, 128), jnp.bfloat16),
            pltpu.VMEM((rows, width), jnp.float32),
            pltpu.VMEM((pairs, rows, 128), jnp.bfloat16),
            pltpu.VMEM((pairs, rows, 128), jnp.bfloat16),
            pltpu.VMEM((pairs, rows, 128), jnp.float32),
            pltpu.SemaphoreType.DMA((2, SPAN, 2)),
            pltpu.SemaphoreType.DMA((2, SPAN, 2)),
        ],
        compiler_params=pltpu.CompilerParams(
            collective_id=0, has_side_effects=True, vmem_limit_bytes=40 << 20
        ),
        name="attention",
    )(normed, embedded, norm_gains, proj_in, proj_out, slot_index[None, :])

    return pl.pallas_call(
        expert_kernel,
        out_shape=jax.ShapeDtypeStruct((rows, width), jnp.bfloat16),
        in_specs=[
            pl.BlockSpec(memory_space=pltpu.SMEM), VMEM, VMEM, VMEM,
            pl.BlockSpec(memory_space=pl.ANY), pl.BlockSpec(memory_space=pl.ANY),
        ],
        out_specs=VMEM,
        scratch_shapes=[
            pltpu.VMEM((width, 2 * hidden_units), jnp.bfloat16),
            pltpu.VMEM((hidden_units, width), jnp.bfloat16),
            pltpu.VMEM((members, capacity, width), jnp.bfloat16),
            pltpu.VMEM((members, capacity, width), jnp.bfloat16),
            pltpu.VMEM((members, capacity, width), jnp.bfloat16),
            pltpu.SemaphoreType.DMA((2,)),
            pltpu.SemaphoreType.DMA((members,)),
            pltpu.SemaphoreType.DMA((members,)),
            pltpu.SemaphoreType.DMA((members,)),
            pltpu.SemaphoreType.DMA((members,)),
        ],
        compiler_params=pltpu.CompilerParams(
            collective_id=1, has_side_effects=True, vmem_limit_bytes=40 << 20
        ),
        name="experts",
    )(
        live_counts, outgoing.reshape(members, capacity, width), slot_index[:, None], hidden,
        expert_in, expert_out,
    )


def solution(mesh):
    in_specs = (
        P("seq"),
        P(("seq", "emb")),
        P(("seq", "emb")),
        P(None, "emb"),
        P(),
        P(),
        P(),
        P("emb", None, None),
        P("emb", None, None),
    )
    out_specs = P(("seq", "emb"), None)
    return jax.shard_map(body, mesh=mesh, in_specs=in_specs, out_specs=out_specs, check_vma=False)
```

time: 328 us -> 194 us (0.59)
  Pallas kernels: 0 us -> 124 us
  matrix products: 90.5 us -> 0 us
  waiting for transfers between devices: 61.7 us -> 14.8 us
  blocking collectives: 41.5 us -> 0 us
  starting transfers between devices: 48 us -> 10.6 us
  local copies, waits for them, and re-layouts: 75.9 us -> 40.1 us
    pallas_call x0 -> x2, Pallas kernels: none -> 124 us  [the longest x1 70.8 us: body(): pl.pallas_call(attention_kernel, out_shape=(jax.ShapeDtypeStruct((rows, w...]
    dot_general x21 -> x0, matrix products: 90.5 us -> none  [the longest x9 56.5 us: attend(): jnp.einsum('hqk,khd->qhd', weights, value_heads, preferred_element_type=j...]
    all_to_all x1 -> x0, blocking collectives: 41.5 us -> none  [body(): lax.all_to_all(outgoing_rows, 'emb', split_axis=0, concat_axis=0, tiled=T...]
    ppermute x8 -> x0, starting transfers between devices: 32.4 us -> none  [shifted(): lax.ppermute(value, axis, [(source, source + steps) for source in range(f...]
    all_to_all x1 -> x0, waiting for transfers between devices: 28.9 us -> none  [body(): lax.all_to_all(finished, 'emb', split_axis=0, concat_axis=0, tiled=True)]
    slice x30 -> x3, local copies, waits for them, and re-layouts: 20.6 us -> 0.22 us  [the longest x8 8.13 us: unpack(): rebuilt[:, model_width:].astype(jnp.bfloat16)]
    ppermute x8 -> x0, waiting for transfers between devices: 18.7 us -> none  [shifted(): lax.ppermute(value, axis, [(source, source + steps) for source in range(f...]
    gather x1, local copies, waits for them, and re-layouts: 32.4 us -> 26.4 us  [body(): columns = table[item_ids]]
  transfers between devices with their start and end apart: 10 -> 1, of which waited for: 6 -> 1; matrix products, arithmetic and copies ran while one was open for 17% -> 1% of each run, Pallas kernels for 0% -> 0%
where the time goes in v1:
time: 194 us; the launch traced here: 193 us
  Pallas kernels  124 us (64%)
  local copies, waits for them, and re-layouts  40.1 us (21%)
  waiting for transfers between devices  14.8 us (8%)
  starting transfers between devices  10.6 us (5%)
  other arithmetic  2.77 us (1%)
    pallas_call x1, Pallas kernels, body(): pl.pallas_call(attention_kernel, out_shape=(jax.ShapeDtypeStruct((rows, w...  70.8 us
    pallas_call x1, Pallas kernels, body(): pl.pallas_call(expert_kernel, out_shape=jax.ShapeDtypeStruct((rows, width...  52.8 us
    gather x1, local copies, waits for them, and re-layouts, body(): columns = table[item_ids]  26.4 us
    all_to_all x1, waiting for transfers between devices, body(): lax.all_to_all(columns, 'emb', split_axis=0, concat_axis=1, tiled=True)  14.8 us
    all_to_all x1, starting transfers between devices, body(): lax.all_to_all(columns, 'emb', split_axis=0, concat_axis=1, tiled=True)  10.6 us
    unnamed x18, local copies, waits for them, and re-layouts  10.6 us
  transfers between devices with their start and end apart: 1, of which 1 were waited for; matrix products, arithmetic and copies ran while one was open for 1% of the time, Pallas kernels for 0%

profile of v1, /device:TPU:12, one launch (start us, length us, event | category | flops | bytes accessed | tf_op | source)
XLA Modules:
  0.0 192.6 jit_solution(14345065363299810099)
XLA Ops:
  0.0 0.0 copy-start.6
  0.0 7.4 %copy.12 = bf16[32768,32]{1,0:T(8,128)(2,1)} copy(bf16[32768,32]{0,1:T(8,128)(2,1)} %param.12) | data formatting | bytes 4194304 | tf_op args[3]
  7.4 0.0 copy-done.6
  7.4 26.4 %gather_fusion = bf16[8192,32]{1,0:T(8,128)(2,1)S(1)} fusion(bf16[32768,32]{1,0:T(8,128)(2,1)} %copy.12, s32[8192]{0:T(1024)S(1)} %fusion), kind=kCustom, calls=%fused_computation | custom fusion | bytes 1081344 | tf_op jit(solution)/shard_map/gather | solution.py:294
  33.8 0.0 copy-start.7
  33.8 1.5 copy.13
  35.3 0.0 slice-start
  35.3 0.0 copy-start.1
  35.3 0.0 copy-start.3
  35.3 0.0 copy-start.4
  35.3 10.6 %all-to-all-start = ((bf16[16,512,32]{1,2,0:T(8,128)(2,1)}), bf16[16,512,32]{1,2,0:T(8,128)(2,1)S(1)}, u32[]{:S(2)}, u32[]{:S(2)}) async-start(bf16[16,512,32]{1,2,0:T(8,128)(2,1)} %copy.13), calls=%async_computation | async-start | bytes 1048576 | tf_op jit(solution)/shard_map/all_to_all | solution.py:295
  46.5 0.0 copy-done.7
  46.5 1.2 reduce-window.6
  47.7 0.2 slice_reduce_fusion
  47.9 0.1 fusion.3
  48.1 0.1 copy.17.slot_ref
  48.2 14.8 %all-to-all-done = bf16[16,512,32]{1,2,0:T(8,128)(2,1)S(1)} async-done(((bf16[16,512,32]{1,2,0:T(8,128)(2,1)}), bf16[16,512,32]{1,2,0:T(8,128)(2,1)S(1)}, u32[]{:S(2)}, u32[]{:S(2)}) %all-to-all-start) | async-done | bytes 524320 | tf_op jit(solution)/shard_map/all_to_all | solution.py:295
  63.0 0.0 copy-start.5
  63.0 0.8 copy-done.5
  63.8 1.3 copy.14.embedded_ref
  65.1 1.2 multiply_reduce_fusion
  66.3 0.0 slice-done
  66.3 0.0 copy-start
  66.3 0.3 multiply_convert_fusion.normed_ref
  66.6 0.0 copy-done.1
  66.6 0.0 copy-done.3
  66.6 0.0 copy-done.4
  66.6 70.8 %attention.1 = (f32[512,512]{1,0:T(8,128)S(1)}, bf16[1024,512]{1,0:T(8,128)(2,1)S(1)}) custom-call(bf16[512,512]{1,0:T(8,128)(2,1)S(1)} %multiply_convert_fusion.normed_ref, bf16[512,512]{1,0:T(8,128)(2,1)S(1)} %copy.14.embedded_ref, f32[3,512]{1,0:T(4,128)S(1)} %copy-done.4, bf16[512,2048]{1,0:T(8,128)(2,1)S(1)} %copy-done.1, ...), custom_call_target="tpu_custom_call" | custom-call | tf_op jit(solution)/shard_map/attention/pallas_call | solution.py:302
  137.4 0.0 copy-done
  137.4 0.0 copy-start.2
  137.4 1.6 copy-done.2
  139.0 52.8 %experts.1 = bf16[512,512]{1,0:T(8,128)(2,1)S(1)} custom-call(s32[1]{0:T(128)} %copy.21.live_ref, bf16[16,64,512]{2,1,0:T(8,128)(2,1)S(1)} %bitcast.31, s32[512,1]{1,0:T(8,128)S(1)} %copy.17.slot_ref, f32[512,512]{1,0:T(8,128)S(1)} %get-tuple-element.8.hidden_ref, bf16[1,512,4096]{2,1,0:T(8,128)(2,1)S(1)} %copy-done, bf16[1,2048,512]{2,1,0:T(8,128)(2,1)S(1)} %copy-done.2), custom_call_target="tpu_custom_call" | custom-call | tf_op jit(solution)/shard_map/experts/pallas_call | solution.py:326
  191.8 0.8 copy.22
  (7 shorter events, 0.1 us)
Async XLA Ops:
  0.0 7.4 %copy-start.6 = (s32[8192]{0:T(1024)S(1)}, s32[8192]{0:T(1024)}, u32[]{:S(2)}) copy-start(s32[8192]{0:T(1024)} %param.9) | copy-start | bytes 98308
  33.8 12.8 %copy-start.7 = (s32[512]{0:T(512)S(1)}, s32[512]{0:T(512)}, u32[]{:S(2)}) copy-start(s32[512]{0:T(512)} %param.10) | copy-start | bytes 6148
  35.3 31.0 %slice-start = ((f32[3,512]{1,0:T(4,128)}), f32[1,512]{1,0:T(1,128)S(1)}, s32[]{:S(2)}) async-start(f32[3,512]{1,0:T(4,128)} %gains_ref.1), calls=%async_computation.1 | async-start | bytes 4096 | tf_op jit(solution)/shard_map/slice | solution.py:298
  35.3 31.3 %copy-start.1 = (bf16[512,2048]{1,0:T(8,128)(2,1)S(1)}, bf16[512,2048]{1,0:T(8,128)(2,1)}, u32[]{:S(2)}) copy-start(bf16[512,2048]{1,0:T(8,128)(2,1)} %proj_in_ref.1) | copy-start | bytes 6291460
  35.3 31.3 %copy-start.3 = (bf16[512,512]{1,0:T(8,128)(2,1)S(1)}, bf16[512,512]{1,0:T(8,128)(2,1)}, u32[]{:S(2)}) copy-start(bf16[512,512]{1,0:T(8,128)(2,1)} %proj_out_ref.1) | copy-start | bytes 1572868
  35.3 31.3 %copy-start.4 = (f32[3,512]{1,0:T(4,128)S(1)}, f32[3,512]{1,0:T(4,128)}, u32[]{:S(2)}) copy-start(f32[3,512]{1,0:T(4,128)} %gains_ref.1) | copy-start | bytes 18436
  35.3 27.8 %all-to-all-start = ((bf16[16,512,32]{1,2,0:T(8,128)(2,1)}), bf16[16,512,32]{1,2,0:T(8,128)(2,1)S(1)}, u32[]{:S(2)}, u32[]{:S(2)}) async-start(bf16[16,512,32]{1,2,0:T(8,128)(2,1)} %copy.13), calls=%async_computation | async-start | bytes 1048576 | tf_op jit(solution)/shard_map/all_to_all | solution.py:295
  63.0 0.8 copy-start.5
  66.3 71.1 %copy-start = (bf16[1,512,4096]{2,1,0:T(8,128)(2,1)S(1)}, bf16[1,512,4096]{2,1,0:T(8,128)(2,1)}, u32[]{:S(2)}) copy-start(bf16[1,512,4096]{2,1,0:T(8,128)(2,1)} %expert_in_ref.1) | copy-start | bytes 12582916
  137.4 1.6 copy-start.2

commit v2 on v1

--- a/solution.py
+++ b/solution.py
@@ -77,15 +77,18 @@
     low_lanes = lax.broadcasted_iota(jnp.int32, (half, 128), 1) < HEAD_DIM
 
     def attend(block, tiles):
-        def project(pair, carry):
+        def project(group, carry):
             for base, held in ((2 * width, keys), (3 * width, values)):
-                columns = pl.ds(pl.multiple_of(base + pair * 128, 128), 128)
+                columns = pl.ds(pl.multiple_of(base + group * 256, 256), 256)
                 found = jnp.dot(block, proj_in_ref[:, columns], preferred_element_type=jnp.float32)
-                held[pair, pl.ds(0, half), :] = jnp.where(low_lanes, found, 0.0).astype(jnp.bfloat16)
-                held[pair, pl.ds(half, half), :] = jnp.where(low_lanes, 0.0, found).astype(jnp.bfloat16)
+                for side in range(2):
+                    pair = 2 * group + side
+                    mine = found[:, side * 128 : (side + 1) * 128]
+                    held[pair, pl.ds(0, half), :] = jnp.where(low_lanes, mine, 0.0).astype(jnp.bfloat16)
+                    held[pair, pl.ds(half, half), :] = jnp.where(low_lanes, 0.0, mine).astype(jnp.bfloat16)
             return carry
 
-        lax.fori_loop(0, pairs, project, 0)
+        lax.fori_loop(0, pairs // 2, project, 0)
 
         def weigh(pair, carry):
             for tile, band in tiles:
@@ -119,12 +122,15 @@
 
     def step(index, carry):
         distance, part = lax.div(index, 2), lax.rem(index, 2)
-        for way in range(2):
-            arrived = halo.at[way, distance, part]
-            transfer(way, distance, part, arrived).wait_recv()
-            transfer(way, distance + 1, part, arrived).start()
-
         def one(way, carry):
+            for side in range(2):
+
+                @pl.when(way == side)
+                def _():
+                    arrived = halo.at[side, distance, part]
+                    transfer(side, distance, part, arrived).wait_recv()
+                    transfer(side, distance + 1, part, arrived).start()
+
             inside = jnp.where(way == 0, me - distance > 0, me + distance < count - 1)
 
             @pl.when(inside)
@@ -274,7 +280,105 @@
         give_back(place).wait_send()
 
 
+def gather_kernel(place_ref, table_ref, outgoing_ref, spread, stage):
+    features, vocabulary = table_ref.shape
+    copies = 128 // features
+    depth = vocabulary // copies
+    members, lines, _ = outgoing_ref.shape
+
+    def arrange(index, carry):
+        start = pl.multiple_of(index * 128, 128)
+        stacked = jnp.concatenate(
+            [table_ref[:, pl.ds(pl.multiple_of(k * depth + start, 128), 128)] for k in range(copies)], axis=0
+        )
+        turned = stacked.astype(jnp.float32).T
+        for shift in range(copies):
+            moved = turned if shift == 0 else pltpu.roll(turned, shift * features, 1)
+            spread[pl.ds(pl.multiple_of(shift * depth + start, 128), 128), :] = moved
+        return carry
+
+    lax.fori_loop(0, depth // 128, arrange, 0)
+
+    lane = lax.broadcasted_iota(jnp.int32, (1, 128), 1)
+    inside = [lane < (k + 1) * features for k in range(copies - 1)]
+
+    def member(target, carry):
+        def eight(index, carry):
+            first = target * (copies * lines) + index * 8
+            for line in range(8):
+                found = [
+                    spread[pl.ds(place_ref[first + k * lines + line], 1), :] for k in range(copies)
+                ]
+                row = found[-1]
+                for k in reversed(range(copies - 1)):
+                    row = jnp.where(inside[k], found[k], row)
+                stage[pl.ds(index * 8 + line, 1), :] = row
+            return carry
+
+        lax.fori_loop(0, lines // 8, eight, 0)
+        outgoing_ref[target] = stage[...].astype(jnp.bfloat16)
+        return carry
+
+    lax.fori_loop(0, members, member, 0)
+
+
+def exchange_kernel(live_ref, outgoing_ref, gains_ref, embedded_ref, normed_ref, inbox, send_sem, recv_sem):
+    members, lines, _ = outgoing_ref.shape
+    width = embedded_ref.shape[1]
+    features = width // members
+    copies = 128 // features
+    group = lax.axis_index("seq")
+    me = lax.axis_index("emb")
+
+    barrier = pltpu.get_barrier_semaphore()
+    for offset in range(1, members):
+        pl.semaphore_signal(
+            barrier, inc=1, device_id=(group, lax.rem(me + offset, members)), device_id_type=MESH
+        )
+    pl.semaphore_wait(barrier, members - 1)
+
+    def transfer(place):
+        target = lax.rem(me + ORDER[place], members)
+        return pltpu.make_async_remote_copy(
+            src_ref=outgoing_ref.at[target],
+            dst_ref=inbox.at[me],
+            send_sem=send_sem.at[place],
+            recv_sem=recv_sem.at[place],
+            device_id=(group, target),
+            device_id_type=MESH,
+        )
+
+    remote = [place for place in range(members) if ORDER[place] != 0]
+    for place in remote:
+        transfer(place).start()
+    inbox[me] = outgoing_ref[me]
+    for place in remote:
+        transfer(place).wait_recv()
+
+    lane = lax.broadcasted_iota(jnp.int32, (lines, 128), 1)
+    row = lax.broadcasted_iota(jnp.int32, (lines, 1), 0)
+    for part in range(copies):
+        blocks = []
+        for column in range(width // 128):
+            joined = None
+            for k in reversed(range(copies)):
+                piece = inbox[column * copies + k].astype(jnp.float32)
+                shift = (k - part) % copies
+                if shift:
+                    piece = pltpu.roll(piece, shift * features, 1)
+                joined = piece if joined is None else jnp.where(lane < (k + 1) * features, piece, joined)
+            blocks.append(joined)
+        values = jnp.concatenate(blocks, axis=1)
+        span = pl.ds(part * lines, lines)
+        embedded_ref[span, :] = values.astype(jnp.bfloat16)
+        live = jnp.where(row + part * lines < live_ref[0], 1.0, 0.0)
+        normed_ref[span, :] = (rms_norm(values, gains_ref[0:1, :]) * live).astype(jnp.bfloat16)
+    for place in remote:
+        transfer(place).wait_send()
+
+
 VMEM = pl.BlockSpec(memory_space=pltpu.VMEM)
+SMEM = pl.BlockSpec(memory_space=pltpu.SMEM)
 
 
 def body(
@@ -291,11 +395,39 @@
     slot_rank = jnp.sum((jnp.cumsum(onehot_domain, axis=0) - onehot_domain) * onehot_domain, axis=1)
     slot_index = domains * capacity + slot_rank
 
-    columns = table[item_ids]
-    embedded = lax.all_to_all(columns, "emb", split_axis=0, concat_axis=1, tiled=True)
-    positions = jnp.arange(rows, dtype=jnp.int32)
-    live_mask = (positions < live_counts[0]).astype(jnp.float32)
-    normed = (rms_norm(embedded.astype(jnp.float32), norm_gains[0]) * live_mask[:, None]).astype(jnp.bfloat16)
+    vocabulary, features = table.shape
+    copies = 128 // features
+    depth = vocabulary // copies
+    lines = rows // copies
+    quarter = (jnp.arange(item_ids.shape[0], dtype=jnp.int32) // lines) % copies
+    place = ((quarter - item_ids // depth) % copies) * depth + item_ids % depth
+    columns = pl.pallas_call(
+        gather_kernel,
+        out_shape=jax.ShapeDtypeStruct((members, lines, 128), jnp.bfloat16),
+        in_specs=[SMEM, VMEM],
+        out_specs=VMEM,
+        scratch_shapes=[
+            pltpu.VMEM((copies * depth, 128), jnp.float32),
+            pltpu.VMEM((lines, 128), jnp.float32),
+        ],
+        compiler_params=pltpu.CompilerParams(vmem_limit_bytes=32 << 20),
+        name="gather",
+    )(place, table.T)
+    embedded, normed = pl.pallas_call(
+        exchange_kernel,
+        out_shape=(jax.ShapeDtypeStruct((rows, width), jnp.bfloat16),) * 2,
+        in_specs=[SMEM, VMEM, VMEM],
+        out_specs=(VMEM, VMEM),
+        scratch_shapes=[
+            pltpu.VMEM((members, lines, 128), jnp.bfloat16),
+            pltpu.SemaphoreType.DMA((members,)),
+            pltpu.SemaphoreType.DMA((members,)),
+        ],
+        compiler_params=pltpu.CompilerParams(
+            collective_id=2, has_side_effects=True, vmem_limit_bytes=40 << 20
+        ),
+        name="exchange",
+    )(live_counts, columns, norm_gains)
 
     half = rows // 2
     pairs = width // 128

time: 194 us -> 171 us (0.88)
  Pallas kernels: 124 us -> 158 us
  local copies, waits for them, and re-layouts: 40.1 us -> 7.15 us
  waiting for transfers between devices: 14.8 us -> 0 us
  starting transfers between devices: 10.6 us -> 0 us
    pallas_call x0 -> x2, Pallas kernels: none -> 44.9 us  [the longest x1 23.7 us: body(): pl.pallas_call(exchange_kernel, out_shape=(jax.ShapeDtypeStruct((rows, wi...]
    gather x1 -> x0, local copies, waits for them, and re-layouts: 26.4 us -> none  [body(): columns = table[item_ids]]
    all_to_all x1 -> x0, waiting for transfers between devices: 14.8 us -> none  [body(): lax.all_to_all(columns, 'emb', split_axis=0, concat_axis=1, tiled=True)]
    pallas_call x1, Pallas kernels: 70.8 us -> 59.8 us  [body(): pl.pallas_call(attention_kernel, out_shape=(jax.ShapeDtypeStruct((rows, w...]
    all_to_all x1 -> x0, starting transfers between devices: 10.6 us -> none  [body(): lax.all_to_all(columns, 'emb', split_axis=0, concat_axis=1, tiled=True)]
    unnamed x18 -> x17, local copies, waits for them, and re-layouts: 10.6 us -> 6.79 us
    all_to_all x2 -> x0, local copies, waits for them, and re-layouts: 2.75 us -> none  [body(): lax.all_to_all(columns, 'emb', split_axis=0, concat_axis=1, tiled=True)]
  transfers between devices with their start and end apart: 1 -> 0, of which waited for: 1 -> 0; matrix products, arithmetic and copies ran while one was open for 1% -> 0% of each run, Pallas kernels for 0% -> 0%
where the time goes in v2:
time: 171 us; the launch traced here: 170 us
  Pallas kernels  158 us (92%)
  local copies, waits for them, and re-layouts  7.15 us (4%)
  other arithmetic  4.15 us (2%)
    pallas_call x1, Pallas kernels, body(): pl.pallas_call(attention_kernel, out_shape=(jax.ShapeDtypeStruct((rows, w...  59.8 us
    pallas_call x1, Pallas kernels, body(): pl.pallas_call(expert_kernel, out_shape=jax.ShapeDtypeStruct((rows, width...  53.2 us
    pallas_call x1, Pallas kernels, body(): pl.pallas_call(exchange_kernel, out_shape=(jax.ShapeDtypeStruct((rows, wi...  23.7 us
    pallas_call x1, Pallas kernels, body(): pl.pallas_call(gather_kernel, out_shape=jax.ShapeDtypeStruct((members, li...  21.2 us
    unnamed x17, local copies, waits for them, and re-layouts  6.79 us

profile of v2, /device:TPU:12, one launch (start us, length us, event | category | flops | bytes accessed | tf_op | source)
XLA Modules:
  0.0 169.9 jit_solution(647417996316132053)
XLA Ops:
  0.0 0.0 copy-start.7
  0.0 0.7 fusion.11
  0.7 1.1 reduce-window.6
  1.8 0.2 slice_reduce_fusion
  2.1 0.8 fusion.9
  2.9 0.7 multiply_add_fusion
  4.2 0.8 fusion.4.place_ref
  5.0 0.0 copy-start.1
  5.0 1.6 copy-done.1
  6.6 0.0 copy-start.2
  6.6 0.0 copy-start.6
  6.6 21.2 %gather.1.outgoing_ref = bf16[16,128,128]{2,1,0:T(8,128)(2,1)S(1)} custom-call(s32[8192]{0:T(1024)S(1)} %fusion.4.place_ref, bf16[32,32768]{1,0:T(8,128)(2,1)S(1)} %bitcast.24), custom_call_target="tpu_custom_call" | custom-call | tf_op jit(solution)/shard_map/gather/pallas_call | solution.py:404
  27.8 0.0 copy-done.7
  27.8 23.7 %exchange.1 = (bf16[512,512]{1,0:T(8,128)(2,1)S(1)}, bf16[512,512]{1,0:T(8,128)(2,1)S(1)}) custom-call(s32[1]{0:T(128)S(6)} %copy.15.live_ref, bf16[16,128,128]{2,1,0:T(8,128)(2,1)S(1)} %gather.1.outgoing_ref, f32[3,512]{1,0:T(4,128)S(1)} %copy-done.7), custom_call_target="tpu_custom_call" | custom-call | tf_op jit(solution)/shard_map/exchange/pallas_call | solution.py:416
  51.5 0.0 copy-start.3
  51.5 0.0 copy-done.2
  51.6 0.0 copy-done.6
  51.6 59.8 %attention.1 = (f32[512,512]{1,0:T(8,128)S(1)}, bf16[1024,512]{1,0:T(8,128)(2,1)S(1)}) custom-call(bf16[512,512]{1,0:T(8,128)(2,1)S(1)} %get-tuple-element.9.normed_ref, bf16[512,512]{1,0:T(8,128)(2,1)S(1)} %get-tuple-element.10.embedded_ref, f32[3,512]{1,0:T(4,128)S(1)} %copy-done.7, bf16[512,2048]{1,0:T(8,128)(2,1)S(1)} %copy-done.2, ...), custom_call_target="tpu_custom_call" | custom-call | tf_op jit(solution)/shard_map/attention/pallas_call | solution.py:434
  111.4 0.0 copy-start.4
  111.4 1.0 copy-done.4
  112.4 0.1 copy.11.slot_ref
  112.5 0.0 copy-done.3
  112.5 0.0 copy-start
  112.5 2.2 %copy-done = bf16[1,512,4096]{2,1,0:T(8,128)(2,1)S(1)} copy-done((bf16[1,512,4096]{2,1,0:T(8,128)(2,1)S(1)}, bf16[1,512,4096]{2,1,0:T(8,128)(2,1)}, u32[]{:S(2)}) %copy-start) | copy-done | bytes 4194328
  114.7 0.0 copy-start.5
  114.7 1.2 copy-done.5
  115.9 53.2 %experts.1 = bf16[512,512]{1,0:T(8,128)(2,1)S(1)} custom-call(s32[1]{0:T(128)S(6)} %copy.15.live_ref, bf16[16,64,512]{2,1,0:T(8,128)(2,1)S(1)} %bitcast.25, s32[512,1]{1,0:T(8,128)S(1)} %copy.11.slot_ref, f32[512,512]{1,0:T(8,128)S(1)} %get-tuple-element.12.hidden_ref, bf16[1,512,4096]{2,1,0:T(8,128)(2,1)S(1)} %copy-done, bf16[1,2048,512]{2,1,0:T(8,128)(2,1)S(1)} %copy-done.3), custom_call_target="tpu_custom_call" | custom-call | tf_op jit(solution)/shard_map/experts/pallas_call | solution.py:458
  169.1 0.8 copy.16
  (2 shorter events, 0.0 us)
Async XLA Ops:
  0.0 27.8 %copy-start.7 = (f32[3,512]{1,0:T(4,128)S(1)}, f32[3,512]{1,0:T(4,128)}, u32[]{:S(2)}) copy-start(f32[3,512]{1,0:T(4,128)} %gains_ref.3) | copy-start | bytes 18436
  5.0 1.6 copy-start.1
  6.6 44.9 %copy-start.2 = (bf16[512,2048]{1,0:T(8,128)(2,1)S(1)}, bf16[512,2048]{1,0:T(8,128)(2,1)}, u32[]{:S(2)}) copy-start(bf16[512,2048]{1,0:T(8,128)(2,1)} %proj_in_ref.1) | copy-start | bytes 6291460
  6.6 44.9 %copy-start.6 = (bf16[512,512]{1,0:T(8,128)(2,1)S(1)}, bf16[512,512]{1,0:T(8,128)(2,1)}, u32[]{:S(2)}) copy-start(bf16[512,512]{1,0:T(8,128)(2,1)} %proj_out_ref.1) | copy-start | bytes 1572868
  51.5 61.0 %copy-start.3 = (bf16[1,2048,512]{2,1,0:T(8,128)(2,1)S(1)}, bf16[1,2048,512]{2,1,0:T(8,128)(2,1)}, u32[]{:S(2)}) copy-start(bf16[1,2048,512]{2,1,0:T(8,128)(2,1)} %expert_out_ref.1) | copy-start | bytes 6291460
  111.4 1.0 copy-start.4
  112.5 2.2 %copy-start = (bf16[1,512,4096]{2,1,0:T(8,128)(2,1)S(1)}, bf16[1,512,4096]{2,1,0:T(8,128)(2,1)}, u32[]{:S(2)}) copy-start(bf16[1,512,4096]{2,1,0:T(8,128)(2,1)} %expert_in_ref.1) | copy-start | bytes 12582916
  114.7 1.2 copy-start.5

commit v3 on v2

--- a/solution.py
+++ b/solution.py
@@ -25,8 +25,22 @@
     return values * (0.5 * jnp.tanh(0.5 * values) + 0.5)
 
 
+def slot_numbers(domains, members, capacity):
+    rows = domains.shape[1]
+    onehot = jnp.where(lax.broadcasted_iota(jnp.int32, (members, rows), 0) == domains, 1.0, 0.0)
+    before = jnp.where(
+        lax.broadcasted_iota(jnp.int32, (rows, rows), 0) < lax.broadcasted_iota(jnp.int32, (rows, rows), 1),
+        1.0, 0.0,
+    )
+    ranks = jnp.dot(
+        onehot.astype(jnp.bfloat16), before.astype(jnp.bfloat16), preferred_element_type=jnp.float32
+    )
+    rank = jnp.sum(ranks * onehot, axis=0, keepdims=True)
+    return domains.astype(jnp.float32) * capacity + rank
+
+
 def attention_kernel(
-    normed_ref, embedded_ref, gains_ref, proj_in_ref, proj_out_ref, slot_ref,
+    normed_ref, embedded_ref, gains_ref, proj_in_ref, proj_out_ref, domains_ref,
     hidden_ref, outgoing_ref,
     halo, queries, gating, keys, values, total, send_sem, recv_sem,
 ):
@@ -74,6 +88,7 @@
         queries[pair] = query * jnp.bfloat16(0.5 / math.sqrt(HEAD_DIM))
         total[pair] = jnp.zeros((rows, 128), jnp.float32)
 
+    slot_row = slot_numbers(domains_ref[...], members, outgoing_ref.shape[0] // members).astype(jnp.int32)
     low_lanes = lax.broadcasted_iota(jnp.int32, (half, 128), 1) < HEAD_DIM
 
     def attend(block, tiles):
@@ -176,29 +191,22 @@
     chunk = 256
     for first in range(0, slots, chunk):
         number = lax.broadcasted_iota(jnp.int32, (chunk, rows), 0) + first
-        chosen = jnp.where(number == slot_ref[...], 1.0, 0.0).astype(jnp.bfloat16)
+        chosen = jnp.where(number == slot_row, 1.0, 0.0).astype(jnp.bfloat16)
         outgoing_ref[pl.ds(first, chunk), :] = jnp.dot(
             chosen, routed, preferred_element_type=jnp.float32
         ).astype(jnp.bfloat16)
 
 
 def expert_kernel(
-    live_ref, outgoing_ref, slot_ref, hidden_ref, expert_in_ref, expert_out_ref,
+    live_ref, outgoing_ref, domains_ref, hidden_ref, expert_in_ref, expert_out_ref,
     mixed_ref,
-    up, down, inbox, finished, returned, load_sem, send_sem, recv_sem, back_send, back_recv,
+    inbox, finished, returned, send_sem, recv_sem, back_send, back_recv,
 ):
     members, capacity, width = outgoing_ref.shape
-    hidden_units = down.shape[0]
+    hidden_units = expert_out_ref.shape[1]
     rows = hidden_ref.shape[0]
     group = lax.axis_index("seq")
     me = lax.axis_index("emb")
-
-    loads = [
-        pltpu.make_async_copy(expert_in_ref.at[0], up, load_sem.at[0]),
-        pltpu.make_async_copy(expert_out_ref.at[0], down, load_sem.at[1]),
-    ]
-    for load in loads:
-        load.start()
 
     barrier = pltpu.get_barrier_semaphore()
     for offset in range(1, members):
@@ -237,8 +245,9 @@
 
     batch = 4
     tile = 256
-    for load in loads:
-        load.wait()
+    slots = slot_numbers(domains_ref[...], members, capacity)
+    same = lax.broadcasted_iota(jnp.int32, (rows, rows), 0) == lax.broadcasted_iota(jnp.int32, (rows, rows), 1)
+    slot_column = jnp.sum(jnp.where(same, slots, 0.0), axis=1, keepdims=True).astype(jnp.int32)
     for first in range(0, members, batch):
         places = [place for place in range(first, first + batch) if place != home]
         for place in places:
@@ -247,14 +256,14 @@
 
         def expert(index, result):
             start = pl.multiple_of(index * tile, tile)
-            gate = jnp.dot(taken, up[:, pl.ds(start, tile)], preferred_element_type=jnp.float32)
+            gate = jnp.dot(taken, expert_in_ref[0, :, pl.ds(start, tile)], preferred_element_type=jnp.float32)
             lift = jnp.dot(
-                taken, up[:, pl.ds(pl.multiple_of(hidden_units + start, tile), tile)],
+                taken, expert_in_ref[0, :, pl.ds(pl.multiple_of(hidden_units + start, tile), tile)],
                 preferred_element_type=jnp.float32,
             )
             activated = (silu(gate) * lift).astype(jnp.bfloat16)
             return result + jnp.dot(
-                activated, down[pl.ds(start, tile), :], preferred_element_type=jnp.float32
+                activated, expert_out_ref[0, pl.ds(start, tile), :], preferred_element_type=jnp.float32
             )
 
         produced = lax.fori_loop(
@@ -269,7 +278,7 @@
         give_back(place).wait_recv()
 
     number = lax.broadcasted_iota(jnp.int32, (rows, members * capacity), 1)
-    chosen = jnp.where(number == slot_ref[...], 1.0, 0.0).astype(jnp.bfloat16)
+    chosen = jnp.where(number == slot_column, 1.0, 0.0).astype(jnp.bfloat16)
     expert_rows = jnp.dot(
         chosen, returned[...].reshape(members * capacity, width), preferred_element_type=jnp.float32
     )
@@ -280,14 +289,20 @@
         give_back(place).wait_send()
 
 
-def gather_kernel(place_ref, table_ref, outgoing_ref, spread, stage):
+def gather_kernel(listed_ref, table_ref, outgoing_ref, place_ref, spread, stage, place_sem):
+    load = pltpu.make_async_copy(listed_ref, place_ref, place_sem)
+    load.start()
     features, vocabulary = table_ref.shape
     copies = 128 // features
     depth = vocabulary // copies
     members, lines, _ = outgoing_ref.shape
 
     def arrange(index, carry):
-        start = pl.multiple_of(index * 128, 128)
+        for step in range(4):
+            turn(pl.multiple_of(index * 512 + step * 128, 128))
+        return carry
+
+    def turn(start):
         stacked = jnp.concatenate(
             [table_ref[:, pl.ds(pl.multiple_of(k * depth + start, 128), 128)] for k in range(copies)], axis=0
         )
@@ -295,27 +310,27 @@
         for shift in range(copies):
             moved = turned if shift == 0 else pltpu.roll(turned, shift * features, 1)
             spread[pl.ds(pl.multiple_of(shift * depth + start, 128), 128), :] = moved
-        return carry
-
-    lax.fori_loop(0, depth // 128, arrange, 0)
+
+    lax.fori_loop(0, depth // 512, arrange, 0)
+    load.wait()
 
     lane = lax.broadcasted_iota(jnp.int32, (1, 128), 1)
     inside = [lane < (k + 1) * features for k in range(copies - 1)]
 
     def member(target, carry):
-        def eight(index, carry):
-            first = target * (copies * lines) + index * 8
-            for line in range(8):
+        def some(index, carry):
+            first = target * (copies * lines) + index * 32
+            for line in range(32):
                 found = [
                     spread[pl.ds(place_ref[first + k * lines + line], 1), :] for k in range(copies)
                 ]
                 row = found[-1]
                 for k in reversed(range(copies - 1)):
                     row = jnp.where(inside[k], found[k], row)
-                stage[pl.ds(index * 8 + line, 1), :] = row
+                stage[pl.ds(index * 32 + line, 1), :] = row
             return carry
 
-        lax.fori_loop(0, lines // 8, eight, 0)
+        lax.fori_loop(0, lines // 32, some, 0)
         outgoing_ref[target] = stage[...].astype(jnp.bfloat16)
         return carry
 
@@ -386,14 +401,9 @@
 ):
     rows = domains.shape[0]
     width = proj_out.shape[0]
-    hidden_units = expert_out.shape[1]
     members = lax.axis_size("emb")
     capacity = 2 * rows // members
     slots = members * capacity
-
-    onehot_domain = (domains[:, None] == jnp.arange(members, dtype=jnp.int32)[None, :]).astype(jnp.int32)
-    slot_rank = jnp.sum((jnp.cumsum(onehot_domain, axis=0) - onehot_domain) * onehot_domain, axis=1)
-    slot_index = domains * capacity + slot_rank
 
     vocabulary, features = table.shape
     copies = 128 // features
@@ -404,11 +414,13 @@
     columns = pl.pallas_call(
         gather_kernel,
         out_shape=jax.ShapeDtypeStruct((members, lines, 128), jnp.bfloat16),
-        in_specs=[SMEM, VMEM],
+        in_specs=[pl.BlockSpec(memory_space=pl.ANY), VMEM],
         out_specs=VMEM,
         scratch_shapes=[
+            pltpu.SMEM(item_ids.shape, jnp.int32),
             pltpu.VMEM((copies * depth, 128), jnp.float32),
             pltpu.VMEM((lines, 128), jnp.float32),
+            pltpu.SemaphoreType.DMA(()),
         ],
         compiler_params=pltpu.CompilerParams(vmem_limit_bytes=32 << 20),
         name="gather",
@@ -424,7 +436,7 @@
             pltpu.SemaphoreType.DMA((members,)),
         ],
         compiler_params=pltpu.CompilerParams(
-            collective_id=2, has_side_effects=True, vmem_limit_bytes=40 << 20
+            collective_id=2, has_side_effects=True, vmem_limit_bytes=12 << 20
         ),
         name="exchange",
     )(live_counts, columns, norm_gains)
@@ -450,37 +462,33 @@
             pltpu.SemaphoreType.DMA((2, SPAN, 2)),
         ],
         compiler_params=pltpu.CompilerParams(
-            collective_id=0, has_side_effects=True, vmem_limit_bytes=40 << 20
+            collective_id=0, has_side_effects=True, vmem_limit_bytes=24 << 20
         ),
         name="attention",
-    )(normed, embedded, norm_gains, proj_in, proj_out, slot_index[None, :])
+    )(normed, embedded, norm_gains, proj_in, proj_out, domains[None, :])
 
     return pl.pallas_call(
         expert_kernel,
         out_shape=jax.ShapeDtypeStruct((rows, width), jnp.bfloat16),
         in_specs=[
-            pl.BlockSpec(memory_space=pltpu.SMEM), VMEM, VMEM, VMEM,
-            pl.BlockSpec(memory_space=pl.ANY), pl.BlockSpec(memory_space=pl.ANY),
+            SMEM, VMEM, VMEM, VMEM, VMEM, VMEM,
         ],
         out_specs=VMEM,
         scratch_shapes=[
-            pltpu.VMEM((width, 2 * hidden_units), jnp.bfloat16),
-            pltpu.VMEM((hidden_units, width), jnp.bfloat16),
             pltpu.VMEM((members, capacity, width), jnp.bfloat16),
             pltpu.VMEM((members, capacity, width), jnp.bfloat16),
             pltpu.VMEM((members, capacity, width), jnp.bfloat16),
-            pltpu.SemaphoreType.DMA((2,)),
             pltpu.SemaphoreType.DMA((members,)),
             pltpu.SemaphoreType.DMA((members,)),
             pltpu.SemaphoreType.DMA((members,)),
             pltpu.SemaphoreType.DMA((members,)),
         ],
         compiler_params=pltpu.CompilerParams(
-            collective_id=1, has_side_effects=True, vmem_limit_bytes=40 << 20
+            collective_id=1, has_side_effects=True, vmem_limit_bytes=24 << 20
         ),
         name="experts",
     )(
-        live_counts, outgoing.reshape(members, capacity, width), slot_index[:, None], hidden,
+        live_counts, outgoing.reshape(members, capacity, width), domains[None, :], hidden,
         expert_in, expert_out,
     )
 

time: 171 us -> 156 us (0.912)
  Pallas kernels: 158 us -> 150 us
  other arithmetic: 4.15 us -> 0.81 us
  local copies, waits for them, and re-layouts: 7.15 us -> 3.99 us
    pallas_call x1, Pallas kernels: 21.2 us -> 11.8 us  [body(): pl.pallas_call(gather_kernel, out_shape=jax.ShapeDtypeStruct((members, li...]
    unnamed x17 -> x15, local copies, waits for them, and re-layouts: 6.79 us -> 3.99 us
where the time goes in v3:
time: 156 us; the launch traced here: 155 us
  Pallas kernels  150 us (96%)
  local copies, waits for them, and re-layouts  3.99 us (3%)
    pallas_call x1, Pallas kernels, body(): pl.pallas_call(attention_kernel, out_shape=(jax.ShapeDtypeStruct((rows, w...  61.3 us
    pallas_call x1, Pallas kernels, body(): pl.pallas_call(expert_kernel, out_shape=jax.ShapeDtypeStruct((rows, width...  52.9 us
    pallas_call x1, Pallas kernels, body(): pl.pallas_call(exchange_kernel, out_shape=(jax.ShapeDtypeStruct((rows, wi...  23.7 us
    pallas_call x1, Pallas kernels, body(): pl.pallas_call(gather_kernel, out_shape=jax.ShapeDtypeStruct((members, li...  11.8 us
    unnamed x15, local copies, waits for them, and re-layouts  3.99 us

profile of v3, /device:TPU:12, one launch (start us, length us, event | category | flops | bytes accessed | tf_op | source)
XLA Modules:
  0.0 155.3 jit_solution(9184642140806814922)
XLA Ops:
  0.0 0.0 copy-start.5
  0.0 0.0 copy-start.6
  0.7 0.8 fusion.4.listed_ref
  1.5 0.0 copy-start.2
  1.5 1.6 %copy-done.2 = bf16[32768,32]{0,1:T(8,128)(2,1)S(1)} copy-done((bf16[32768,32]{0,1:T(8,128)(2,1)S(1)}, bf16[32768,32]{0,1:T(8,128)(2,1)}, u32[]{:S(2)}) %copy-start.2) | copy-done | bytes 2097176
  3.1 0.0 copy-start.4
  3.1 0.0 copy-start.1
  3.1 11.8 %gather.1.outgoing_ref = bf16[16,128,128]{2,1,0:T(8,128)(2,1)S(1)} custom-call(s32[8192]{0:T(1024)S(1)} %fusion.4.listed_ref, bf16[32,32768]{1,0:T(8,128)(2,1)S(1)} %bitcast.3), custom_call_target="tpu_custom_call" | custom-call | tf_op jit(solution)/shard_map/gather/pallas_call | solution.py:414
  14.9 0.0 copy-done.5
  15.0 0.0 copy-start
  15.0 23.7 %exchange.1 = (bf16[512,512]{1,0:T(8,128)(2,1)S(1)}, bf16[512,512]{1,0:T(8,128)(2,1)S(1)}) custom-call(s32[1]{0:T(128)S(6)} %copy.11.live_ref, bf16[16,128,128]{2,1,0:T(8,128)(2,1)S(1)} %gather.1.outgoing_ref, f32[3,512]{1,0:T(4,128)S(1)} %copy-done.5), custom_call_target="tpu_custom_call" | custom-call | tf_op jit(solution)/shard_map/exchange/pallas_call | solution.py:428
  38.7 0.0 copy-done.6
  38.7 0.0 copy-done.4
  38.7 0.0 copy-start.3
  38.7 1.6 %copy-done.3 = bf16[512,2048]{1,0:T(8,128)(2,1)S(1)} copy-done((bf16[512,2048]{1,0:T(8,128)(2,1)S(1)}, bf16[512,2048]{1,0:T(8,128)(2,1)}, u32[]{:S(2)}) %copy-start.3) | copy-done | bytes 2097176
  40.3 61.3 %attention.1 = (f32[512,512]{1,0:T(8,128)S(1)}, bf16[1024,512]{1,0:T(8,128)(2,1)S(1)}) custom-call(bf16[512,512]{1,0:T(8,128)(2,1)S(1)} %get-tuple-element.9.normed_ref, bf16[512,512]{1,0:T(8,128)(2,1)S(1)} %get-tuple-element.10.embedded_ref, f32[3,512]{1,0:T(4,128)S(1)} %copy-done.5, bf16[512,2048]{1,0:T(8,128)(2,1)S(1)} %copy-done.3, ...), custom_call_target="tpu_custom_call" | custom-call | tf_op jit(solution)/shard_map/attention/pallas_call | solution.py:446
  101.6 0.0 copy-done.1
  101.6 0.0 copy-done
  101.6 52.9 %experts.1 = bf16[512,512]{1,0:T(8,128)(2,1)S(1)} custom-call(s32[1]{0:T(128)S(6)} %copy.11.live_ref, bf16[16,64,512]{2,1,0:T(8,128)(2,1)S(1)} %bitcast.4, s32[1,512]{1,0:T(1,128)S(1)} %bitcast.6, f32[512,512]{1,0:T(8,128)S(1)} %get-tuple-element.12.hidden_ref, bf16[1,512,4096]{2,1,0:T(8,128)(2,1)S(1)} %copy-done, bf16[1,2048,512]{2,1,0:T(8,128)(2,1)S(1)} %copy-done.1), custom_call_target="tpu_custom_call" | custom-call | tf_op jit(solution)/shard_map/experts/pallas_call | solution.py:470
  154.5 0.8 copy.12
Async XLA Ops:
  0.0 14.9 %copy-start.5 = (f32[3,512]{1,0:T(4,128)S(1)}, f32[3,512]{1,0:T(4,128)}, u32[]{:S(2)}) copy-start(f32[3,512]{1,0:T(4,128)} %gains_ref.3) | copy-start | bytes 18436
  0.0 38.7 %copy-start.6 = (s32[512]{0:T(512)S(1)}, s32[512]{0:T(512)}, u32[]{:S(2)}) copy-start(s32[512]{0:T(512)} %param.10) | copy-start | bytes 6148
  1.5 1.6 %copy-start.2 = (bf16[32768,32]{0,1:T(8,128)(2,1)S(1)}, bf16[32768,32]{0,1:T(8,128)(2,1)}, u32[]{:S(2)}) copy-start(bf16[32768,32]{0,1:T(8,128)(2,1)} %param.12) | copy-start | bytes 6291460
  3.1 35.6 %copy-start.4 = (bf16[512,512]{1,0:T(8,128)(2,1)S(1)}, bf16[512,512]{1,0:T(8,128)(2,1)}, u32[]{:S(2)}) copy-start(bf16[512,512]{1,0:T(8,128)(2,1)} %proj_out_ref.1) | copy-start | bytes 1572868
  3.1 98.5 %copy-start.1 = (bf16[1,2048,512]{2,1,0:T(8,128)(2,1)S(1)}, bf16[1,2048,512]{2,1,0:T(8,128)(2,1)}, u32[]{:S(2)}) copy-start(bf16[1,2048,512]{2,1,0:T(8,128)(2,1)} %expert_out_ref.1) | copy-start | bytes 6291460
  15.0 86.7 %copy-start = (bf16[1,512,4096]{2,1,0:T(8,128)(2,1)S(1)}, bf16[1,512,4096]{2,1,0:T(8,128)(2,1)}, u32[]{:S(2)}) copy-start(bf16[1,512,4096]{2,1,0:T(8,128)(2,1)} %expert_in_ref.1) | copy-start | bytes 12582916
  38.7 1.6 %copy-start.3 = (bf16[512,2048]{1,0:T(8,128)(2,1)S(1)}, bf16[512,2048]{1,0:T(8,128)(2,1)}, u32[]{:S(2)}) copy-start(bf16[512,2048]{1,0:T(8,128)(2,1)} %proj_in_ref.1) | copy-start | bytes 6291460

commit v4 on v3

--- a/solution.py
+++ b/solution.py
@@ -137,15 +137,12 @@
 
     def step(index, carry):
         distance, part = lax.div(index, 2), lax.rem(index, 2)
+        for way in range(2):
+            arrived = halo.at[way, distance, part]
+            transfer(way, distance, part, arrived).wait_recv()
+            transfer(way, distance + 1, part, arrived).start()
+
         def one(way, carry):
-            for side in range(2):
-
-                @pl.when(way == side)
-                def _():
-                    arrived = halo.at[side, distance, part]
-                    transfer(side, distance, part, arrived).wait_recv()
-                    transfer(side, distance + 1, part, arrived).start()
-
             inside = jnp.where(way == 0, me - distance > 0, me + distance < count - 1)
 
             @pl.when(inside)

time: 156 us -> 156 us (level)
  no operation moved by 1% of the time
where the time goes in v4:
time: 156 us; the launch traced here: 155 us
  Pallas kernels  150 us (96%)
  local copies, waits for them, and re-layouts  3.99 us (3%)
    pallas_call x1, Pallas kernels, body(): pl.pallas_call(attention_kernel, out_shape=(jax.ShapeDtypeStruct((rows, w...  61.1 us
    pallas_call x1, Pallas kernels, body(): pl.pallas_call(expert_kernel, out_shape=jax.ShapeDtypeStruct((rows, width...  52.9 us
    pallas_call x1, Pallas kernels, body(): pl.pallas_call(exchange_kernel, out_shape=(jax.ShapeDtypeStruct((rows, wi...  23.7 us
    pallas_call x1, Pallas kernels, body(): pl.pallas_call(gather_kernel, out_shape=jax.ShapeDtypeStruct((members, li...  11.8 us
    unnamed x15, local copies, waits for them, and re-layouts  3.99 us

profile of v4, /device:TPU:12, one launch (start us, length us, event | category | flops | bytes accessed | tf_op | source)
XLA Modules:
  0.0 155.1 jit_solution(10472894730994535947)
XLA Ops:
  0.0 0.0 copy-start.5
  0.0 0.0 copy-start.6
  0.7 0.8 fusion.4.listed_ref
  1.5 0.0 copy-start.2
  1.5 1.6 %copy-done.2 = bf16[32768,32]{0,1:T(8,128)(2,1)S(1)} copy-done((bf16[32768,32]{0,1:T(8,128)(2,1)S(1)}, bf16[32768,32]{0,1:T(8,128)(2,1)}, u32[]{:S(2)}) %copy-start.2) | copy-done | bytes 2097176
  3.1 0.0 copy-start.4
  3.1 0.0 copy-start.1
  3.1 11.8 %gather.1.outgoing_ref = bf16[16,128,128]{2,1,0:T(8,128)(2,1)S(1)} custom-call(s32[8192]{0:T(1024)S(1)} %fusion.4.listed_ref, bf16[32,32768]{1,0:T(8,128)(2,1)S(1)} %bitcast.3), custom_call_target="tpu_custom_call" | custom-call | tf_op jit(solution)/shard_map/gather/pallas_call | solution.py:411
  14.9 0.0 copy-done.5
  15.0 0.0 copy-start
  15.0 23.7 %exchange.1 = (bf16[512,512]{1,0:T(8,128)(2,1)S(1)}, bf16[512,512]{1,0:T(8,128)(2,1)S(1)}) custom-call(s32[1]{0:T(128)S(6)} %copy.11.live_ref, bf16[16,128,128]{2,1,0:T(8,128)(2,1)S(1)} %gather.1.outgoing_ref, f32[3,512]{1,0:T(4,128)S(1)} %copy-done.5), custom_call_target="tpu_custom_call" | custom-call | tf_op jit(solution)/shard_map/exchange/pallas_call | solution.py:425
  38.7 0.0 copy-done.6
  38.7 0.0 copy-done.4
  38.7 0.0 copy-start.3
  38.7 1.6 %copy-done.3 = bf16[512,2048]{1,0:T(8,128)(2,1)S(1)} copy-done((bf16[512,2048]{1,0:T(8,128)(2,1)S(1)}, bf16[512,2048]{1,0:T(8,128)(2,1)}, u32[]{:S(2)}) %copy-start.3) | copy-done | bytes 2097176
  40.3 61.1 %attention.1 = (f32[512,512]{1,0:T(8,128)S(1)}, bf16[1024,512]{1,0:T(8,128)(2,1)S(1)}) custom-call(bf16[512,512]{1,0:T(8,128)(2,1)S(1)} %get-tuple-element.9.normed_ref, bf16[512,512]{1,0:T(8,128)(2,1)S(1)} %get-tuple-element.10.embedded_ref, f32[3,512]{1,0:T(4,128)S(1)} %copy-done.5, bf16[512,2048]{1,0:T(8,128)(2,1)S(1)} %copy-done.3, ...), custom_call_target="tpu_custom_call" | custom-call | tf_op jit(solution)/shard_map/attention/pallas_call | solution.py:443
  101.4 0.0 copy-done.1
  101.4 0.0 copy-done
  101.4 52.9 %experts.1 = bf16[512,512]{1,0:T(8,128)(2,1)S(1)} custom-call(s32[1]{0:T(128)S(6)} %copy.11.live_ref, bf16[16,64,512]{2,1,0:T(8,128)(2,1)S(1)} %bitcast.4, s32[1,512]{1,0:T(1,128)S(1)} %bitcast.6, f32[512,512]{1,0:T(8,128)S(1)} %get-tuple-element.12.hidden_ref, bf16[1,512,4096]{2,1,0:T(8,128)(2,1)S(1)} %copy-done, bf16[1,2048,512]{2,1,0:T(8,128)(2,1)S(1)} %copy-done.1), custom_call_target="tpu_custom_call" | custom-call | tf_op jit(solution)/shard_map/experts/pallas_call | solution.py:467
  154.3 0.8 copy.12
Async XLA Ops:
  0.0 14.9 %copy-start.5 = (f32[3,512]{1,0:T(4,128)S(1)}, f32[3,512]{1,0:T(4,128)}, u32[]{:S(2)}) copy-start(f32[3,512]{1,0:T(4,128)} %gains_ref.3) | copy-start | bytes 18436
  0.0 38.7 %copy-start.6 = (s32[512]{0:T(512)S(1)}, s32[512]{0:T(512)}, u32[]{:S(2)}) copy-start(s32[512]{0:T(512)} %param.10) | copy-start | bytes 6148
  1.5 1.6 %copy-start.2 = (bf16[32768,32]{0,1:T(8,128)(2,1)S(1)}, bf16[32768,32]{0,1:T(8,128)(2,1)}, u32[]{:S(2)}) copy-start(bf16[32768,32]{0,1:T(8,128)(2,1)} %param.12) | copy-start | bytes 6291460
  3.1 35.6 %copy-start.4 = (bf16[512,512]{1,0:T(8,128)(2,1)S(1)}, bf16[512,512]{1,0:T(8,128)(2,1)}, u32[]{:S(2)}) copy-start(bf16[512,512]{1,0:T(8,128)(2,1)} %proj_out_ref.1) | copy-start | bytes 1572868
  3.1 98.3 %copy-start.1 = (bf16[1,2048,512]{2,1,0:T(8,128)(2,1)S(1)}, bf16[1,2048,512]{2,1,0:T(8,128)(2,1)}, u32[]{:S(2)}) copy-start(bf16[1,2048,512]{2,1,0:T(8,128)(2,1)} %expert_out_ref.1) | copy-start | bytes 6291460
  15.0 86.4 %copy-start = (bf16[1,512,4096]{2,1,0:T(8,128)(2,1)S(1)}, bf16[1,512,4096]{2,1,0:T(8,128)(2,1)}, u32[]{:S(2)}) copy-start(bf16[1,512,4096]{2,1,0:T(8,128)(2,1)} %expert_in_ref.1) | copy-start | bytes 12582916
  38.7 1.6 %copy-start.3 = (bf16[512,2048]{1,0:T(8,128)(2,1)S(1)}, bf16[512,2048]{1,0:T(8,128)(2,1)}, u32[]{:S(2)}) copy-start(bf16[512,2048]{1,0:T(8,128)(2,1)} %proj_in_ref.1) | copy-start | bytes 6291460
